TPU v7x, 32 devices: a whole 2x2x4 slice. The times are simulated.
32 devices in a mesh: seq: 4 (over y, core), head: 8 (over z, x).
Axes of the slice: x: 2, y: 2, z: 4, core: 2. Of those that a mesh axis runs over, the one named last changes fastest.
Arguments:
- query: bfloat16 [4096, 4096], P(('seq', 'head')), may hold values from -6 to 6
- key_matrix: bfloat16 [4096, 2048], P(('seq', 'head')), may hold values from -6 to 6
- value_matrix: bfloat16 [4096, 2048], P(('seq', 'head')), may hold values from -6 to 6
- output_gradient: bfloat16 [4096, 4096], P(('seq', 'head')), may hold values from -6 to 6
- attn_out: bfloat16 [4096, 4096], P(('seq', 'head')), may hold values from -3 to 3
- doc_offsets: int32 [9], replicated, may hold values from 0 to 4096, as said below
- stats: float32 [4096, 32], P(('seq', 'head')), may hold values from -1 to 9
Outputs:
- grad_query: bfloat16 [4096, 4096], P(('seq', 'head'))
- key_gradient: bfloat16 [4096, 2048], P(('seq', 'head'))
- value_gradient: bfloat16 [4096, 2048], P(('seq', 'head'))
Inputs may be any that keep to these rules, and one draw needn't show every extreme that they name: doc_offsets[0] is 0, doc_offsets[8] is 4096, the entries rise strictly; no document has more than 1023 tokens and one has exactly that many.
All inputs are finite; a program needn't handle non-finite values.
Results may differ from a plain program's by a relative error of at most 0.0063.
Values may be sent and summed in bfloat16 or wider, within the bound.
A program may use at most 64 MiB of HBM per device.

v0:
```python
import jax
import jax.numpy as jnp
from jax import lax
from jax.sharding import PartitionSpec as P

HQ = 32
HEAD_SIZE = 128
DOCHALF = 512
QBLK = 512


attn_scale = 144.0 ** (-0.5)


def partner(value, axis, apart):
    mask = 2**apart
    pairs = [(source, source ^ mask) for source in range(lax.axis_size(axis))]
    return lax.ppermute(value, axis, pairs)


def from_behind(value, axis, steps):
    count = lax.axis_size(axis)
    leading, last = (max(0, -steps), min(count, count - steps))
    return lax.ppermute(value, axis, [(source, source + steps) for source in range(leading, last)])


def tile_grads(query_rows, grad_rows, lse_rows, delta_rows, key_window, value_window, allowed):
    score = (
        jnp.einsum("qgrd,kgd->grqk", query_rows, key_window, preferred_element_type=jnp.float32)
        * attn_scale
    )
    norm_stat = jnp.transpose(lse_rows, (1, 2, 0))[..., None]
    prob = jnp.where(allowed[None, None], jnp.exp(score - norm_stat), 0.0)
    dprob = jnp.einsum(
        "qgrd,kgd->grqk", grad_rows, value_window, preferred_element_type=jnp.float32
    )
    dscore = prob * (dprob - jnp.transpose(delta_rows, (1, 2, 0))[..., None])
    prob_low = prob.astype(jnp.bfloat16)
    dscore_low = dscore.astype(jnp.bfloat16)
    value_gradient = jnp.einsum(
        "grqk,qgrd->kgd", prob_low, grad_rows, preferred_element_type=jnp.float32
    )
    key_gradient = (
        jnp.einsum("grqk,qgrd->kgd", dscore_low, query_rows, preferred_element_type=jnp.float32)
        * attn_scale
    )
    grad_query = (
        jnp.einsum("grqk,kgd->qgrd", dscore_low, key_window, preferred_element_type=jnp.float32)
        * attn_scale
    )
    return (grad_query, key_gradient, value_gradient)


def doc_numbers(positions, inner):
    return jnp.sum((inner[None, :] <= positions[:, None]).astype(jnp.int32), axis=1)


def shards(query, key_matrix, value_matrix, output_gradient, attn_out, doc_offsets, stats):
    token_count_local = query.shape[0]
    members = lax.axis_size("head")
    group_span = token_count_local * members
    per_device = HQ // members
    lookback = 2 * DOCHALF
    width = lookback + QBLK
    group = lax.axis_index("seq")
    member = lax.axis_index("head")
    parity = member % 2
    half_width = HEAD_SIZE // 2
    delta_correction = jnp.sum(
        (output_gradient.astype(jnp.float32) * attn_out.astype(jnp.float32)).reshape(
            token_count_local, HQ, HEAD_SIZE
        ),
        axis=2,
    )
    query_heads, grad_heads = (
        lax.all_to_all(query, "head", split_axis=1, concat_axis=0, tiled=True),
        lax.all_to_all(output_gradient, "head", split_axis=1, concat_axis=0, tiled=True),
    )
    lse_heads, delta_heads = (
        lax.all_to_all(stats, "head", split_axis=1, concat_axis=0, tiled=True),
        lax.all_to_all(delta_correction, "head", split_axis=1, concat_axis=0, tiled=True),
    )
    key_cols, value_cols = (
        lax.all_to_all(key_matrix, "head", split_axis=1, concat_axis=0, tiled=True),
        lax.all_to_all(value_matrix, "head", split_axis=1, concat_axis=0, tiled=True),
    )
    if per_device >= 2:
        groups = per_device // 2
        key_heads = key_cols.reshape(group_span, groups, HEAD_SIZE)
        value_heads = value_cols.reshape(group_span, groups, HEAD_SIZE)
    else:
        groups = 1
        other_key, other_value = partner((key_cols, value_cols), "head", 0)
        key_heads = jnp.where(
            parity == 0,
            jnp.concatenate([key_cols, other_key], 1),
            jnp.concatenate([other_key, key_cols], 1),
        ).reshape(group_span, 1, HEAD_SIZE)
        value_heads = jnp.where(
            parity == 0,
            jnp.concatenate([value_cols, other_value], 1),
            jnp.concatenate([other_value, value_cols], 1),
        ).reshape(group_span, 1, HEAD_SIZE)
    repeats = per_device // groups
    query_heads = query_heads.reshape(group_span, groups, repeats, HEAD_SIZE)
    grad_heads = grad_heads.reshape(group_span, groups, repeats, HEAD_SIZE)
    lse_heads = lse_heads.reshape(group_span, groups, repeats)
    delta_heads = delta_heads.reshape(group_span, groups, repeats)
    prior_key, prior_value = from_behind(
        (key_heads[group_span - lookback :], value_heads[group_span - lookback :]), "seq", 1
    )
    key_ext = jnp.concatenate([prior_key, key_heads], 0)
    value_ext = jnp.concatenate([prior_value, value_heads], 0)
    inner = doc_offsets[1:-1]
    query_pos = group * group_span + jnp.arange(group_span, dtype=jnp.int32)
    key_pos = group * group_span - lookback + jnp.arange(lookback + group_span, dtype=jnp.int32)
    query_doc = doc_numbers(query_pos, inner)
    key_doc = doc_numbers(key_pos, inner)

    def block_step(block, carry):
        grad_q, grad_k, grad_v = carry
        start = (block * QBLK).astype(jnp.int32)
        query_rows = lax.dynamic_slice_in_dim(query_heads, start, QBLK, 0)
        grad_rows = lax.dynamic_slice_in_dim(grad_heads, start, QBLK, 0)
        lse_rows = lax.dynamic_slice_in_dim(lse_heads, start, QBLK, 0)
        delta_rows = lax.dynamic_slice_in_dim(delta_heads, start, QBLK, 0)
        key_window = lax.dynamic_slice_in_dim(key_ext, start, width, 0)
        value_window = lax.dynamic_slice_in_dim(value_ext, start, width, 0)
        rows_pos = lax.dynamic_slice_in_dim(query_pos, start, QBLK, 0)
        rows_doc = lax.dynamic_slice_in_dim(query_doc, start, QBLK, 0)
        cols_pos = lax.dynamic_slice_in_dim(key_pos, start, width, 0)
        cols_doc = lax.dynamic_slice_in_dim(key_doc, start, width, 0)
        allowed = (
            (cols_doc[None, :] == rows_doc[:, None])
            & (cols_pos[None, :] <= rows_pos[:, None])
            & (cols_pos[None, :] >= 0)
        )
        block_q, block_k, block_v = tile_grads(
            query_rows, grad_rows, lse_rows, delta_rows, key_window, value_window, allowed
        )
        grad_q = lax.dynamic_update_slice_in_dim(grad_q, block_q, start, 0)
        grad_k = lax.dynamic_update_slice_in_dim(
            grad_k, lax.dynamic_slice_in_dim(grad_k, start, width, 0) + block_k, start, 0
        )
        grad_v = lax.dynamic_update_slice_in_dim(
            grad_v, lax.dynamic_slice_in_dim(grad_v, start, width, 0) + block_v, start, 0
        )
        return (grad_q, grad_k, grad_v)

    init = (
        jnp.zeros((group_span, groups, repeats, HEAD_SIZE), jnp.float32),
        jnp.zeros((lookback + group_span, groups, HEAD_SIZE), jnp.float32),
        jnp.zeros((lookback + group_span, groups, HEAD_SIZE), jnp.float32),
    )
    grad_q, grad_k, grad_v = lax.fori_loop(0, group_span // QBLK, block_step, init)
    back_key, back_value = (
        from_behind(grad_k[:lookback].astype(jnp.bfloat16), "seq", -1).astype(jnp.float32),
        from_behind(grad_v[:lookback].astype(jnp.bfloat16), "seq", -1).astype(jnp.float32),
    )
    own_key = grad_k[lookback:].at[group_span - lookback :].add(back_key)
    own_value = grad_v[lookback:].at[group_span - lookback :].add(back_value)
    query_low = grad_q.astype(jnp.bfloat16).reshape(group_span, per_device * HEAD_SIZE)
    grad_query = lax.all_to_all(query_low, "head", split_axis=0, concat_axis=1, tiled=True)
    if per_device >= 2:
        send_key = own_key.reshape(group_span, groups * HEAD_SIZE)
        send_value = own_value.reshape(group_span, groups * HEAD_SIZE)
    else:
        flat_key = own_key.reshape(group_span, HEAD_SIZE)
        flat_value = own_value.reshape(group_span, HEAD_SIZE)
        keep_key = lax.dynamic_slice_in_dim(flat_key, parity * half_width, half_width, 1)
        keep_value = lax.dynamic_slice_in_dim(flat_value, parity * half_width, half_width, 1)
        give_key = lax.dynamic_slice_in_dim(flat_key, (1 - parity) * half_width, half_width, 1)
        give_value = lax.dynamic_slice_in_dim(flat_value, (1 - parity) * half_width, half_width, 1)
        from_key, from_value = partner((give_key, give_value), "head", 0)
        send_key = keep_key + from_key
        send_value = keep_value + from_value
    key_gradient_summed, value_gradient_summed = (
        lax.all_to_all(
            send_key.astype(jnp.bfloat16), "head", split_axis=0, concat_axis=1, tiled=True
        ).astype(send_key.dtype),
        lax.all_to_all(
            send_value.astype(jnp.bfloat16), "head", split_axis=0, concat_axis=1, tiled=True
        ).astype(send_value.dtype),
    )
    key_gradient = key_gradient_summed.astype(jnp.bfloat16)
    value_gradient = value_gradient_summed.astype(jnp.bfloat16)
    return (grad_query, key_gradient, value_gradient)


def solution(mesh):
    placed = (
        P(("seq", "head"), None),
        P(("seq", "head"), None),
        P(("seq", "head"), None),
        P(("seq", "head"), None),
        P(("seq", "head"), None),
        P(),
        P(("seq", "head"), None),
    )
    return jax.shard_map(
        shards,
        mesh=mesh,
        in_specs=placed,
        out_specs=(P(("seq", "head"), None), P(("seq", "head"), None), P(("seq", "head"), None)),
        check_vma=False,
    )
```

profile of v0, /device:TPU:4, one launch (start us, length us, event | category | flops | bytes accessed | tf_op | source)
XLA Modules:
  0.0 238.3 jit_solution(3520835461747851998)
XLA Ops:
  0.6 5.8 %all-to-all-start.2 = ((f32[128,8,4]{0,2,1:T(4,128)}), f32[128,8,4]{0,2,1:T(4,128)S(1)}, u32[]{:S(2)}, u32[]{:S(2)}) async-start(f32[128,8,4]{0,2,1:T(4,128)} %bitcast.171), calls=%async_computation.2 | async-start | bytes 32768 | tf_op jit(solution)/shard_map/all_to_all | solution.py:80
  6.4 1.8 multiply_bitcast_fusion
  9.9 3.1 %all-to-all-done.2 = f32[128,8,4]{0,2,1:T(4,128)S(1)} async-done(((f32[128,8,4]{0,2,1:T(4,128)}), f32[128,8,4]{0,2,1:T(4,128)S(1)}, u32[]{:S(2)}, u32[]{:S(2)}) %all-to-all-start.2) | async-done | bytes 16416 | tf_op jit(solution)/shard_map/all_to_all | solution.py:80
  13.0 3.3 %all-to-all-start.5 = ((f32[128,8,4]{0,2,1:T(4,128)}), f32[128,8,4]{0,2,1:T(4,128)S(1)}, u32[]{:S(2)}, u32[]{:S(2)}) async-start(f32[128,8,4]{0,2,1:T(4,128)} %bitcast.26), calls=%async_computation.5 | async-start | bytes 32768 | tf_op jit(solution)/shard_map/all_to_all | solution.py:81
  16.4 2.0 copy.116
  18.4 4.5 %all-to-all-done.5 = f32[128,8,4]{0,2,1:T(4,128)S(1)} async-done(((f32[128,8,4]{0,2,1:T(4,128)}), f32[128,8,4]{0,2,1:T(4,128)S(1)}, u32[]{:S(2)}, u32[]{:S(2)}) %all-to-all-start.5) | async-done | bytes 16416 | tf_op jit(solution)/shard_map/all_to_all | solution.py:81
  22.9 3.5 %all-to-all-start = ((bf16[128,8,256]{0,2,1:T(8,128)(2,1)}), bf16[128,8,256]{0,2,1:T(8,128)(2,1)S(1)}, u32[]{:S(2)}, u32[]{:S(2)}) async-start(bf16[128,8,256]{0,2,1:T(8,128)(2,1)} %bitcast.16), calls=%async_computation | async-start | bytes 1048576 | tf_op jit(solution)/shard_map/all_to_all | solution.py:84
  26.4 2.1 copy.121
  28.5 10.2 %all-to-all-done = bf16[128,8,256]{0,2,1:T(8,128)(2,1)S(1)} async-done(((bf16[128,8,256]{0,2,1:T(8,128)(2,1)}), bf16[128,8,256]{0,2,1:T(8,128)(2,1)S(1)}, u32[]{:S(2)}, u32[]{:S(2)}) %all-to-all-start) | async-done | bytes 524320 | tf_op jit(solution)/shard_map/all_to_all | solution.py:84
  38.7 3.6 %all-to-all-start.3 = ((bf16[128,8,256]{0,2,1:T(8,128)(2,1)}), bf16[128,8,256]{0,2,1:T(8,128)(2,1)S(1)}, u32[]{:S(2)}, u32[]{:S(2)}) async-start(bf16[128,8,256]{0,2,1:T(8,128)(2,1)} %bitcast.22), calls=%async_computation.3 | async-start | bytes 1048576 | tf_op jit(solution)/shard_map/all_to_all | solution.py:85
  43.7 12.1 %all-to-all-done.3 = bf16[128,8,256]{0,2,1:T(8,128)(2,1)S(1)} async-done(((bf16[128,8,256]{0,2,1:T(8,128)(2,1)}), bf16[128,8,256]{0,2,1:T(8,128)(2,1)S(1)}, u32[]{:S(2)}, u32[]{:S(2)}) %all-to-all-start.3) | async-done | bytes 524320 | tf_op jit(solution)/shard_map/all_to_all | solution.py:85
  56.6 3.7 %all-to-all-start.1 = ((bf16[128,8,512]{0,2,1:T(8,128)(2,1)}), bf16[128,8,512]{0,2,1:T(8,128)(2,1)S(1)}, u32[]{:S(2)}, u32[]{:S(2)}) async-start(bf16[128,8,512]{0,2,1:T(8,128)(2,1)} %bitcast.18), calls=%async_computation.1 | async-start | bytes 2097152 | tf_op jit(solution)/shard_map/all_to_all | solution.py:76
  61.6 23.9 %all-to-all-done.1 = bf16[128,8,512]{0,2,1:T(8,128)(2,1)S(1)} async-done(((bf16[128,8,512]{0,2,1:T(8,128)(2,1)}), bf16[128,8,512]{0,2,1:T(8,128)(2,1)S(1)}, u32[]{:S(2)}, u32[]{:S(2)}) %all-to-all-start.1) | async-done | bytes 1048608 | tf_op jit(solution)/shard_map/all_to_all | solution.py:76
  85.5 3.7 %all-to-all-start.4 = ((bf16[128,8,512]{0,2,1:T(8,128)(2,1)}), bf16[128,8,512]{0,2,1:T(8,128)(2,1)S(1)}, u32[]{:S(2)}, u32[]{:S(2)}) async-start(bf16[128,8,512]{0,2,1:T(8,128)(2,1)} %bitcast.24), calls=%async_computation.4 | async-start | bytes 2097152 | tf_op jit(solution)/shard_map/all_to_all | solution.py:77
  89.2 1.4 copy.122
  91.6 1.9 collective-permute-start.1
  94.2 2.1 collective-permute-start
  96.6 5.8 %collective-permute-done.1 = bf16[1024,2,128]{0,2,1:T(8,128)(2,1)} collective-permute-done((bf16[1024,2,128]{0,2,1:T(8,128)(2,1)}, bf16[1024,2,128]{0,2,1:T(8,128)(2,1)}, u32[]{:S(2)}, u32[]{:S(2)}) %collective-permute-start.1) | collective-permute-done | bytes 524320 | tf_op jit(solution)/shard_map/ppermute | solution.py:24
  102.4 2.3 pad_maximum_fusion.1
  104.7 3.3 %collective-permute-done = bf16[1024,2,128]{0,2,1:T(8,128)(2,1)} collective-permute-done((bf16[1024,2,128]{0,2,1:T(8,128)(2,1)S(1)}, bf16[1024,2,128]{0,2,1:T(8,128)(2,1)}, u32[]{:S(2)}, u32[]{:S(2)}) %collective-permute-start) | collective-permute-done | bytes 524320 | tf_op jit(solution)/shard_map/ppermute | solution.py:24
  109.3 1.6 copy.119
  111.0 2.3 reshape.216
  113.3 1.7 all-to-all-done.4
  118.1 1.5 broadcast.179.clone
  119.8 48.6 %while.21 = (s32[]{:T(128)}, bf16[1024,2,2,128]{0,3,2,1:T(8,128)(2,1)}, f32[2048,2,128]{0,2,1:T(8,128)S(1)}, f32[2048,2,128]{0,2,1:T(8,128)}, bf16[2048,2,128]{0...) while((s32[]{:T(128)}, ...), condition=%wide.region_4.5_spmd, body=%wide.region_3.4_spmd.sunk | while | flops 4062578176 | bytes 158969360 | solution.py:155
  120.2 1.5 and_and_fusion.2
  121.7 3.0 %fusion.68 = f32[2,1536,512,2]{2,1,3,0:T(8,128)S(1)} fusion(bf16[2048,2,128]{0,2,1:T(8,128)(2,1)S(1)} %get-tuple-element.520, s32[]{:T(128)S(6)} %select_n.54, bf16[1024,2,2,128]{0,3,2,1:T(8,128)(2,1)} %get-tuple-element.525, s32[]{:T(128)S(6)} %select_n.53), kind=kOutput, calls=%fused_computation.21.clone.1 | convolution fusion | flops 805306368 | bytes 13893640 | tf_op jit(solution)/shard_map/while/body/eval_jaxpr/qgrd,kgd->grqk/dot_general | solution.py:29
  124.7 4.5 %copy-done = f32[2,1536,512,2]{2,1,3,0:T(8,128)} copy-done((f32[2,1536,512,2]{2,1,3,0:T(8,128)}, f32[2,1536,512,2]{2,1,3,0:T(8,128)S(1)}, u32[]{:S(2)}) %copy-start) | copy-done | bytes 12582936 | tf_op jit(solution)/shard_map/while
  129.3 3.2 %fusion.72 = f32[2048,2,128]{0,2,1:T(8,128)S(1)} fusion(f32[2048,2,128]{0,2,1:T(8,128)S(1)} %copy-done.2, s32[]{:T(128)S(6)} %select_n.54, f32[2,1536,512,2]{2,1,3,0:T(8,128)S(1)} %fusion.68, f32[2,2,512]{2,1,0:T(2,128)S(1)} %get-tuple-element.475, pred[512,1536]{0,1:T(8,128)(4,1)S(1)} %and_and_fusion.2, ...), kind=kOutput, calls=%fused_computation.12.clone.1 | convolution fusion | flops 818282496 | bytes 17047560 | tf_op jit(solution)/shard_map/while/body/eval_jaxpr/grqk,qgrd->kgd/dot_general | solution.py:40
  132.5 8.1 %fusion.69 = bf16[2,2,512,1536]{2,3,1,0:T(8,128)(2,1)S(1)} fusion(f32[2,1536,512,2]{2,1,3,0:T(8,128)} %copy-done, f32[2,2,512]{2,1,0:T(2,128)S(1)} %get-tuple-element.474, f32[2,2,512]{2,1,0:T(2,128)S(1)} %get-tuple-element.475, pred[512,1536]{0,1:T(8,128)(4,1)S(1)} %and_and_fusion.2, bf16[2048,2,128]{0,2,1:T(8,128)(2,1)S(1)} %copy-done.13, ...), kind=kOutput, calls=%fused_computation.2.clone.1 | convolution fusion | flops 824180736 | bytes 20987912 | tf_op jit(solution)/shard_map/while/body/eval_jaxpr/qgrd,kgd->grqk/dot_general | solution.py:34
  141.8 2.3 fusion.71
  144.5 1.5 and_and_fusion.2
  146.0 3.0 %fusion.68 = f32[2,1536,512,2]{2,1,3,0:T(8,128)S(1)} fusion(bf16[2048,2,128]{0,2,1:T(8,128)(2,1)S(1)} %get-tuple-element.520, s32[]{:T(128)S(6)} %select_n.54, bf16[1024,2,2,128]{0,3,2,1:T(8,128)(2,1)} %get-tuple-element.525, s32[]{:T(128)S(6)} %select_n.53), kind=kOutput, calls=%fused_computation.21.clone.1 | convolution fusion | flops 805306368 | bytes 13893640 | tf_op jit(solution)/shard_map/while/body/eval_jaxpr/qgrd,kgd->grqk/dot_general | solution.py:29
  149.1 4.5 %copy-done = f32[2,1536,512,2]{2,1,3,0:T(8,128)} copy-done((f32[2,1536,512,2]{2,1,3,0:T(8,128)}, f32[2,1536,512,2]{2,1,3,0:T(8,128)S(1)}, u32[]{:S(2)}) %copy-start) | copy-done | bytes 12582936 | tf_op jit(solution)/shard_map/while
  153.6 3.2 %fusion.72 = f32[2048,2,128]{0,2,1:T(8,128)S(1)} fusion(f32[2048,2,128]{0,2,1:T(8,128)S(1)} %copy-done.2, s32[]{:T(128)S(6)} %select_n.54, f32[2,1536,512,2]{2,1,3,0:T(8,128)S(1)} %fusion.68, f32[2,2,512]{2,1,0:T(2,128)S(1)} %get-tuple-element.475, pred[512,1536]{0,1:T(8,128)(4,1)S(1)} %and_and_fusion.2, ...), kind=kOutput, calls=%fused_computation.12.clone.1 | convolution fusion | flops 818282496 | bytes 17047560 | tf_op jit(solution)/shard_map/while/body/eval_jaxpr/grqk,qgrd->kgd/dot_general | solution.py:40
  156.8 8.1 %fusion.69 = bf16[2,2,512,1536]{2,3,1,0:T(8,128)(2,1)S(1)} fusion(f32[2,1536,512,2]{2,1,3,0:T(8,128)} %copy-done, f32[2,2,512]{2,1,0:T(2,128)S(1)} %get-tuple-element.474, f32[2,2,512]{2,1,0:T(2,128)S(1)} %get-tuple-element.475, pred[512,1536]{0,1:T(8,128)(4,1)S(1)} %and_and_fusion.2, bf16[2048,2,128]{0,2,1:T(8,128)(2,1)S(1)} %copy-done.13, ...), kind=kOutput, calls=%fused_computation.2.clone.1 | convolution fusion | flops 824180736 | bytes 20987912 | tf_op jit(solution)/shard_map/while/body/eval_jaxpr/qgrd,kgd->grqk/dot_general | solution.py:34
  166.1 2.3 fusion.71
  168.5 2.1 collective-permute-start.2
  170.7 6.5 %collective-permute-done.2 = bf16[1024,2,128]{0,2,1:T(8,128)(2,1)S(1)} collective-permute-done((bf16[1024,2,128]{0,2,1:T(8,128)(2,1)S(1)}, bf16[1024,2,128]{0,2,1:T(8,128)(2,1)S(1)}, u32[]{:S(2)}, u32[]{:S(2)}) %collective-permute-start.2) | collective-permute-done | bytes 524320 | tf_op jit(solution)/shard_map/ppermute | solution.py:24
  178.5 4.2 %all-to-all-start.7 = ((bf16[8,128,256]{2,1,0:T(8,128)(2,1)}), bf16[8,128,256]{2,1,0:T(8,128)(2,1)S(1)}, u32[]{:S(2)}, u32[]{:S(2)}) async-start(bf16[8,128,256]{2,1,0:T(8,128)(2,1)} %copy.153), calls=%async_computation.7 | async-start | bytes 1048576 | tf_op jit(solution)/shard_map/all_to_all | solution.py:178
  182.7 1.4 slice.66
  184.1 3.5 %collective-permute-start.3 = (bf16[1024,2,128]{0,2,1:T(8,128)(2,1)S(1)}, bf16[1024,2,128]{0,2,1:T(8,128)(2,1)S(1)}, u32[]{:S(2)}, u32[]{:S(2)}) collective-permute-start(bf16[1024,2,128]{0,2,1:T(8,128)(2,1)S(1)} %slice.66), channel_id=1, source_target_pairs={{8,0},{16,8},{24,16},{9,1},{17,9},{25,17},{10,2},{18,10},{26,18},{... | collective-permute-start | bytes 1572872 | tf_op jit(solution)/shard_map/ppermute | solution.py:24
  187.7 6.7 %collective-permute-done.3 = bf16[1024,2,128]{0,2,1:T(8,128)(2,1)S(1)} collective-permute-done((bf16[1024,2,128]{0,2,1:T(8,128)(2,1)S(1)}, bf16[1024,2,128]{0,2,1:T(8,128)(2,1)S(1)}, u32[]{:S(2)}, u32[]{:S(2)}) %collective-permute-start.3) | collective-permute-done | bytes 524320 | tf_op jit(solution)/shard_map/ppermute | solution.py:24
  197.0 5.7 %all-to-all-start.8 = ((bf16[8,128,256]{2,1,0:T(8,128)(2,1)}), bf16[8,128,256]{2,1,0:T(8,128)(2,1)S(1)}, u32[]{:S(2)}, u32[]{:S(2)}) async-start(bf16[8,128,256]{2,1,0:T(8,128)(2,1)} %copy.154), calls=%async_computation.8 | async-start | bytes 1048576 | tf_op jit(solution)/shard_map/all_to_all | solution.py:181
  203.0 1.5 copy.152
  204.4 8.8 %all-to-all-done.8 = bf16[8,128,256]{2,1,0:T(8,128)(2,1)S(1)} async-done(((bf16[8,128,256]{2,1,0:T(8,128)(2,1)}), bf16[8,128,256]{2,1,0:T(8,128)(2,1)S(1)}, u32[]{:S(2)}, u32[]{:S(2)}) %all-to-all-start.8) | async-done | bytes 524320 | tf_op jit(solution)/shard_map/all_to_all | solution.py:181
  213.2 6.5 %all-to-all-start.6 = ((bf16[8,128,512]{2,1,0:T(8,128)(2,1)}), bf16[8,128,512]{2,1,0:T(8,128)(2,1)S(1)}, u32[]{:S(2)}, u32[]{:S(2)}) async-start(bf16[8,128,512]{2,1,0:T(8,128)(2,1)} %copy.152), calls=%async_computation.6 | async-start | bytes 2097152 | tf_op jit(solution)/shard_map/all_to_all | solution.py:163
  222.3 13.9 %all-to-all-done.6 = bf16[8,128,512]{2,1,0:T(8,128)(2,1)S(1)} async-done(((bf16[8,128,512]{2,1,0:T(8,128)(2,1)}), bf16[8,128,512]{2,1,0:T(8,128)(2,1)S(1)}, u32[]{:S(2)}, u32[]{:S(2)}) %all-to-all-start.6) | async-done | bytes 1048608 | tf_op jit(solution)/shard_map/all_to_all | solution.py:163
  (95 shorter events, 23.5 us)
Async XLA Ops:
  0.6 12.4 %all-to-all-start.2 = ((f32[128,8,4]{0,2,1:T(4,128)}), f32[128,8,4]{0,2,1:T(4,128)S(1)}, u32[]{:S(2)}, u32[]{:S(2)}) async-start(f32[128,8,4]{0,2,1:T(4,128)} %bitcast.171), calls=%async_computation.2 | async-start | bytes 32768 | tf_op jit(solution)/shard_map/all_to_all | solution.py:80
  8.6 33.8 %copy-start.12 = (bf16[128,4096]{1,0:T(8,128)(2,1)S(1)}, bf16[128,4096]{1,0:T(8,128)(2,1)}, u32[]{:S(2)}) copy-start(bf16[128,4096]{1,0:T(8,128)(2,1)} %param.17) | copy-start | bytes 3145732
  13.0 9.9 %all-to-all-start.5 = ((f32[128,8,4]{0,2,1:T(4,128)}), f32[128,8,4]{0,2,1:T(4,128)S(1)}, u32[]{:S(2)}, u32[]{:S(2)}) async-start(f32[128,8,4]{0,2,1:T(4,128)} %bitcast.26), calls=%async_computation.5 | async-start | bytes 32768 | tf_op jit(solution)/shard_map/all_to_all | solution.py:81
  22.9 15.8 %all-to-all-start = ((bf16[128,8,256]{0,2,1:T(8,128)(2,1)}), bf16[128,8,256]{0,2,1:T(8,128)(2,1)S(1)}, u32[]{:S(2)}, u32[]{:S(2)}) async-start(bf16[128,8,256]{0,2,1:T(8,128)(2,1)} %bitcast.16), calls=%async_computation | async-start | bytes 1048576 | tf_op jit(solution)/shard_map/all_to_all | solution.py:84
  26.4 33.9 %copy-start.7 = (bf16[128,4096]{1,0:T(8,128)(2,1)S(1)}, bf16[128,4096]{1,0:T(8,128)(2,1)}, u32[]{:S(2)}) copy-start(bf16[128,4096]{1,0:T(8,128)(2,1)} %param.20) | copy-start | bytes 3145732
  38.7 17.1 %copy-start.8 = (bf16[128,8,256]{0,2,1:T(8,128)(2,1)}, bf16[128,8,256]{0,2,1:T(8,128)(2,1)S(1)}, u32[]{:S(2)}) copy-start(bf16[128,8,256]{0,2,1:T(8,128)(2,1)S(1)} %all-to-all-done) | copy-start | bytes 1572868
  38.7 17.1 %all-to-all-start.3 = ((bf16[128,8,256]{0,2,1:T(8,128)(2,1)}), bf16[128,8,256]{0,2,1:T(8,128)(2,1)S(1)}, u32[]{:S(2)}, u32[]{:S(2)}) async-start(bf16[128,8,256]{0,2,1:T(8,128)(2,1)} %bitcast.22), calls=%async_computation.3 | async-start | bytes 1048576 | tf_op jit(solution)/shard_map/all_to_all | solution.py:85
  55.8 0.8 copy-start.10
  56.6 28.9 %all-to-all-start.1 = ((bf16[128,8,512]{0,2,1:T(8,128)(2,1)}), bf16[128,8,512]{0,2,1:T(8,128)(2,1)S(1)}, u32[]{:S(2)}, u32[]{:S(2)}) async-start(bf16[128,8,512]{0,2,1:T(8,128)(2,1)} %bitcast.18), calls=%async_computation.1 | async-start | bytes 2097152 | tf_op jit(solution)/shard_map/all_to_all | solution.py:76
  61.6 31.9 %copy-start.9 = (bf16[128,8,256]{0,2,1:T(8,128)(2,1)S(1)}, bf16[128,8,256]{0,2,1:T(8,128)(2,1)}, u32[]{:S(2)}) copy-start(bf16[128,8,256]{0,2,1:T(8,128)(2,1)} %copy-done.8) | copy-start | bytes 1572868
  85.5 10.8 %copy-start.15 = (s32[9]{0:T(128)S(1)}, s32[9]{0:T(128)}, u32[]{:S(2)}) copy-start(s32[9]{0:T(128)} %param.22) | copy-start | bytes 112
  85.5 29.5 %all-to-all-start.4 = ((bf16[128,8,512]{0,2,1:T(8,128)(2,1)}), bf16[128,8,512]{0,2,1:T(8,128)(2,1)S(1)}, u32[]{:S(2)}, u32[]{:S(2)}) async-start(bf16[128,8,512]{0,2,1:T(8,128)(2,1)} %bitcast.24), calls=%async_computation.4 | async-start | bytes 2097152 | tf_op jit(solution)/shard_map/all_to_all | solution.py:77
  91.6 10.8 %collective-permute-start.1 = (bf16[1024,2,128]{0,2,1:T(8,128)(2,1)}, bf16[1024,2,128]{0,2,1:T(8,128)(2,1)}, u32[]{:S(2)}, u32[]{:S(2)}) collective-permute-start(bf16[1024,2,128]{0,2,1:T(8,128)(2,1)} %reshape.218), channel_id=1, source_target_pairs={{0,8},{8,16},{16,24},{1,9},{9,17},{17,25},{2,10},{10,18},{18,26},{... | collective-permute-start | bytes 1572872 | tf_op jit(solution)/shard_map/ppermute | solution.py:24
  94.1 10.6 %copy-start.11 = (bf16[1024,2,128]{0,2,1:T(8,128)(2,1)}, bf16[1024,2,128]{0,2,1:T(8,128)(2,1)S(1)}, u32[]{:S(2)}) copy-start(bf16[1024,2,128]{0,2,1:T(8,128)(2,1)S(1)} %reshape.215) | copy-start | bytes 1572868
  94.2 13.9 %collective-permute-start = (bf16[1024,2,128]{0,2,1:T(8,128)(2,1)S(1)}, bf16[1024,2,128]{0,2,1:T(8,128)(2,1)}, u32[]{:S(2)}, u32[]{:S(2)}) collective-permute-start(bf16[1024,2,128]{0,2,1:T(8,128)(2,1)S(1)} %reshape.215), channel_id=1, source_target_pairs={{0,8},{8,16},{16,24},{1,9},{9,17},{17,25},{2,10},{10,18},{18,26},{... | collective-permute-start | bytes 1572872 | tf_op jit(solution)/shard_map/ppermute | solution.py:24
  121.7 7.6 %copy-start.2 = (f32[2048,2,128]{0,2,1:T(8,128)S(1)}, f32[2048,2,128]{0,2,1:T(8,128)}, u32[]{:S(2)}) copy-start(f32[2048,2,128]{0,2,1:T(8,128)} %get-tuple-element.500) | copy-start | bytes 6291460 | tf_op jit(solution)/shard_map/while
  121.7 7.6 %copy-start.14 = (bf16[1024,2,2,128]{0,3,2,1:T(8,128)(2,1)S(1)}, bf16[1024,2,2,128]{0,3,2,1:T(8,128)(2,1)}, u32[]{:S(2)}) copy-start(bf16[1024,2,2,128]{0,3,2,1:T(8,128)(2,1)} %get-tuple-element.528) | copy-start | bytes 3145732 | tf_op jit(solution)/shard_map/while
  124.7 4.5 %copy-start = (f32[2,1536,512,2]{2,1,3,0:T(8,128)}, f32[2,1536,512,2]{2,1,3,0:T(8,128)S(1)}, u32[]{:S(2)}) copy-start(f32[2,1536,512,2]{2,1,3,0:T(8,128)S(1)} %fusion.68) | copy-start | bytes 37748740 | tf_op jit(solution)/shard_map/while
  129.3 3.2 %copy-start.13 = (bf16[2048,2,128]{0,2,1:T(8,128)(2,1)S(1)}, bf16[2048,2,128]{0,2,1:T(8,128)(2,1)}, u32[]{:S(2)}) copy-start(bf16[2048,2,128]{0,2,1:T(8,128)(2,1)} %get-tuple-element.527) | copy-start | bytes 3145732 | tf_op jit(solution)/shard_map/while
  132.5 8.1 %copy-start.3 = (f32[2048,2,128]{0,2,1:T(8,128)}, f32[2048,2,128]{0,2,1:T(8,128)S(1)}, u32[]{:S(2)}) copy-start(f32[2048,2,128]{0,2,1:T(8,128)S(1)} %fusion.72) | copy-start | bytes 6291460 | tf_op jit(solution)/shard_map/while
  132.5 8.1 %copy-start.4 = (bf16[1024,2,2,128]{0,3,2,1:T(8,128)(2,1)S(1)}, bf16[1024,2,2,128]{0,3,2,1:T(8,128)(2,1)}, u32[]{:S(2)}) copy-start(bf16[1024,2,2,128]{0,3,2,1:T(8,128)(2,1)} %get-tuple-element.498) | copy-start | bytes 3145732 | tf_op jit(solution)/shard_map/while
  140.6 1.2 copy-start.1
  141.8 2.3 copy-start.5
  146.0 7.6 %copy-start.2 = (f32[2048,2,128]{0,2,1:T(8,128)S(1)}, f32[2048,2,128]{0,2,1:T(8,128)}, u32[]{:S(2)}) copy-start(f32[2048,2,128]{0,2,1:T(8,128)} %get-tuple-element.500) | copy-start | bytes 6291460 | tf_op jit(solution)/shard_map/while
  146.0 7.6 %copy-start.14 = (bf16[1024,2,2,128]{0,3,2,1:T(8,128)(2,1)S(1)}, bf16[1024,2,2,128]{0,3,2,1:T(8,128)(2,1)}, u32[]{:S(2)}) copy-start(bf16[1024,2,2,128]{0,3,2,1:T(8,128)(2,1)} %get-tuple-element.528) | copy-start | bytes 3145732 | tf_op jit(solution)/shard_map/while
  149.1 4.5 %copy-start = (f32[2,1536,512,2]{2,1,3,0:T(8,128)}, f32[2,1536,512,2]{2,1,3,0:T(8,128)S(1)}, u32[]{:S(2)}) copy-start(f32[2,1536,512,2]{2,1,3,0:T(8,128)S(1)} %fusion.68) | copy-start | bytes 37748740 | tf_op jit(solution)/shard_map/while
  153.6 3.2 %copy-start.13 = (bf16[2048,2,128]{0,2,1:T(8,128)(2,1)S(1)}, bf16[2048,2,128]{0,2,1:T(8,128)(2,1)}, u32[]{:S(2)}) copy-start(bf16[2048,2,128]{0,2,1:T(8,128)(2,1)} %get-tuple-element.527) | copy-start | bytes 3145732 | tf_op jit(solution)/shard_map/while
  156.8 8.1 %copy-start.3 = (f32[2048,2,128]{0,2,1:T(8,128)}, f32[2048,2,128]{0,2,1:T(8,128)S(1)}, u32[]{:S(2)}) copy-start(f32[2048,2,128]{0,2,1:T(8,128)S(1)} %fusion.72) | copy-start | bytes 6291460 | tf_op jit(solution)/shard_map/while
  156.8 8.1 %copy-start.4 = (bf16[1024,2,2,128]{0,3,2,1:T(8,128)(2,1)S(1)}, bf16[1024,2,2,128]{0,3,2,1:T(8,128)(2,1)}, u32[]{:S(2)}) copy-start(bf16[1024,2,2,128]{0,3,2,1:T(8,128)(2,1)} %get-tuple-element.498) | copy-start | bytes 3145732 | tf_op jit(solution)/shard_map/while
  164.9 1.2 copy-start.1
  166.1 2.3 copy-start.5
  168.5 8.6 %collective-permute-start.2 = (bf16[1024,2,128]{0,2,1:T(8,128)(2,1)S(1)}, bf16[1024,2,128]{0,2,1:T(8,128)(2,1)S(1)}, u32[]{:S(2)}, u32[]{:S(2)}) collective-permute-start(bf16[1024,2,128]{0,2,1:T(8,128)(2,1)S(1)} %slice.67), channel_id=1, source_target_pairs={{8,0},{16,8},{24,16},{9,1},{17,9},{25,17},{10,2},{18,10},{26,18},{... | collective-permute-start | bytes 1572872 | tf_op jit(solution)/shard_map/ppermute | solution.py:24
  178.5 18.4 %all-to-all-start.7 = ((bf16[8,128,256]{2,1,0:T(8,128)(2,1)}), bf16[8,128,256]{2,1,0:T(8,128)(2,1)S(1)}, u32[]{:S(2)}, u32[]{:S(2)}) async-start(bf16[8,128,256]{2,1,0:T(8,128)(2,1)} %copy.153), calls=%async_computation.7 | async-start | bytes 1048576 | tf_op jit(solution)/shard_map/all_to_all | solution.py:178
  182.7 19.9 %copy-start.6 = (bf16[1024,2,2,128]{0,3,2,1:T(8,128)(2,1)S(1)}, bf16[1024,2,2,128]{0,3,2,1:T(8,128)(2,1)}, u32[]{:S(2)}) copy-start(bf16[1024,2,2,128]{0,3,2,1:T(8,128)(2,1)} %get-tuple-element.274) | copy-start | bytes 3145732
  184.1 10.2 %collective-permute-start.3 = (bf16[1024,2,128]{0,2,1:T(8,128)(2,1)S(1)}, bf16[1024,2,128]{0,2,1:T(8,128)(2,1)S(1)}, u32[]{:S(2)}, u32[]{:S(2)}) collective-permute-start(bf16[1024,2,128]{0,2,1:T(8,128)(2,1)S(1)} %slice.66), channel_id=1, source_target_pairs={{8,0},{16,8},{24,16},{9,1},{17,9},{25,17},{10,2},{18,10},{26,18},{... | collective-permute-start | bytes 1572872 | tf_op jit(solution)/shard_map/ppermute | solution.py:24
  197.0 16.2 %all-to-all-start.8 = ((bf16[8,128,256]{2,1,0:T(8,128)(2,1)}), bf16[8,128,256]{2,1,0:T(8,128)(2,1)S(1)}, u32[]{:S(2)}, u32[]{:S(2)}) async-start(bf16[8,128,256]{2,1,0:T(8,128)(2,1)} %copy.154), calls=%async_computation.8 | async-start | bytes 1048576 | tf_op jit(solution)/shard_map/all_to_all | solution.py:181
  213.2 23.1 %all-to-all-start.6 = ((bf16[8,128,512]{2,1,0:T(8,128)(2,1)}), bf16[8,128,512]{2,1,0:T(8,128)(2,1)S(1)}, u32[]{:S(2)}, u32[]{:S(2)}) async-start(bf16[8,128,512]{2,1,0:T(8,128)(2,1)} %copy.152), calls=%async_computation.6 | async-start | bytes 2097152 | tf_op jit(solution)/shard_map/all_to_all | solution.py:163
where the time goes:
time: 243 us; the launch traced here: 238 us
  waiting for transfers between devices  100 us (41%)
  starting transfers between devices  49.8 us (20%)
  local copies, waits for them, and re-layouts  40.6 us (17%)
  matrix products  35.3 us (15%)
  other arithmetic  10.8 us (4%)
    all_to_all x1, waiting for transfers between devices, shards(): lax.all_to_all(query, 'head', split_axis=1, concat_axis=0, tiled=True)  23.9 us
    ppermute x4, waiting for transfers between devices, from_behind(): lax.ppermute(value, axis, [(source, source + steps) for source in range(l...  22.3 us
    dot_general x2, matrix products, tile_grads(): jnp.einsum('qgrd,kgd->grqk', grad_rows, value_window, preferred_element_t...  16.2 us
    all_to_all x1, waiting for transfers between devices, shards(): lax.all_to_all(query_low, 'head', split_axis=0, concat_axis=1, tiled=True)  13.9 us
    all_to_all x1, waiting for transfers between devices, shards(): lax.all_to_all(value_matrix, 'head', split_axis=1, concat_axis=0, tiled=T...  12.1 us
    unnamed x27, local copies, waits for them, and re-layouts  11.8 us
    all_to_all x1, waiting for transfers between devices, shards(): lax.all_to_all(key_matrix, 'head', split_axis=1, concat_axis=0, tiled=True)  10.2 us
    ppermute x4, starting transfers between devices, from_behind(): lax.ppermute(value, axis, [(source, source + steps) for source in range(l...  9.69 us
  transfers between devices with their start and end apart: 13, of which 12 were waited for; matrix products, arithmetic and copies ran while one was open for 12% of the time, Pallas kernels for 0%

commit v1 on v0

--- a/solution.py
+++ b/solution.py
@@ -1,6 +1,11 @@
+import functools
+import math
+
 import jax
 import jax.numpy as jnp
 from jax import lax
+from jax.experimental import pallas as pl
+from jax.experimental.pallas import tpu as pltpu
 from jax.sharding import PartitionSpec as P
 
 HQ = 32
@@ -187,6 +192,325 @@
     return (grad_query, key_gradient, value_gradient)
 
 
+TOKENS = 128
+TILE = 256
+MESH = pl.DeviceIdType.MESH
+
+
+def wait_bytes(ref, sem):
+    pltpu.make_async_copy(ref, ref, sem).wait()
+
+
+def greet_all(groups, members, group, member):
+    barrier = pltpu.get_barrier_semaphore()
+    everyone = groups * members
+
+    @pl.loop(1, everyone)
+    def _(apart):
+        to_group = lax.rem(group + apart // members, groups)
+        to_member = lax.rem(member + lax.rem(apart, members), members)
+        pl.semaphore_signal(barrier, inc=1, device_id=(to_group, to_member), device_id_type=MESH)
+
+    pl.semaphore_wait(barrier, everyone - 1)
+
+
+def spread_kernel(
+    groups,
+    members,
+    query,
+    grad,
+    key,
+    value,
+    stat,
+    query_all,
+    grad_all,
+    key_all,
+    value_all,
+    stat_all,
+    send_sem,
+    recv_sem,
+):
+    half = members // 2
+    everyone = groups * members
+    group = lax.axis_index("seq")
+    member = lax.axis_index("head")
+    side = member // half
+    greet_all(groups, members, group, member)
+    token_row = pl.multiple_of((group * members + member) * TOKENS, TOKENS)
+    side_slot = group * half + lax.rem(member, half)
+    side_row = pl.multiple_of(side_slot * TOKENS, TOKENS)
+
+    def pieces(slot):
+        narrow = pl.ds(pl.multiple_of(slot * HEAD_SIZE, HEAD_SIZE), HEAD_SIZE)
+        wide = pl.ds(pl.multiple_of(slot * 2 * HEAD_SIZE, 2 * HEAD_SIZE), 2 * HEAD_SIZE)
+        far = (
+            (key.at[:, narrow], key_all.at[pl.ds(token_row, TOKENS)], 0),
+            (value.at[:, narrow], value_all.at[pl.ds(token_row, TOKENS)], 1),
+        )
+        near = (
+            (query.at[:, wide], query_all.at[pl.ds(side_row, TOKENS)], 2),
+            (grad.at[:, wide], grad_all.at[pl.ds(side_row, TOKENS)], 3),
+            (stat.at[slot], stat_all.at[side_slot], 4),
+        )
+        return far, near
+
+    def send(piece, to_group, to_member):
+        source, target, which = piece
+        pltpu.make_async_remote_copy(
+            src_ref=source,
+            dst_ref=target,
+            send_sem=send_sem.at[which],
+            recv_sem=recv_sem.at[which],
+            device_id=(to_group, to_member),
+            device_id_type=MESH,
+        ).start()
+
+    @pl.loop(1, everyone)
+    def _(apart):
+        to_group = lax.rem(group + apart // members, groups)
+        to_member = lax.rem(member + lax.rem(apart, members), members)
+        slot = to_group * half + lax.rem(to_member, half)
+        far, near = pieces(slot)
+        for piece in far:
+            send(piece, to_group, to_member)
+
+        @pl.when(to_member // half == side)
+        def _():
+            for piece in near:
+                send(piece, to_group, to_member)
+
+    far, near = pieces(side_slot)
+    for source, target, which in far + near:
+        pltpu.make_async_copy(source, target, recv_sem.at[which]).start()
+    others = (everyone - 1) * TOKENS
+    near_others = (groups * half - 1) * TOKENS
+    wait_bytes(key_all.at[pl.ds(0, others)], send_sem.at[0])
+    wait_bytes(value_all.at[pl.ds(0, others)], send_sem.at[1])
+    wait_bytes(query_all.at[pl.ds(0, near_others)], send_sem.at[2])
+    wait_bytes(grad_all.at[pl.ds(0, near_others)], send_sem.at[3])
+    wait_bytes(stat_all.at[pl.ds(0, groups * half - 1)], send_sem.at[4])
+    for which, ref in enumerate((key_all, value_all, query_all, grad_all, stat_all)):
+        wait_bytes(ref, recv_sem.at[which])
+
+
+def collect_kernel(
+    groups,
+    members,
+    grad_q,
+    grad_k,
+    grad_v,
+    query_out,
+    key_out,
+    value_out,
+    send_sem,
+    recv_sem,
+):
+    half = members // 2
+    everyone = groups * members
+    group = lax.axis_index("seq")
+    member = lax.axis_index("head")
+    side = member // half
+    greet_all(groups, members, group, member)
+    my_slot = group * half + lax.rem(member, half)
+    narrow = pl.ds(pl.multiple_of(my_slot * HEAD_SIZE, HEAD_SIZE), HEAD_SIZE)
+    wide = pl.ds(pl.multiple_of(my_slot * 2 * HEAD_SIZE, 2 * HEAD_SIZE), 2 * HEAD_SIZE)
+
+    def pieces(to_group, to_member):
+        row = pl.multiple_of((to_group * members + to_member) * TOKENS, TOKENS)
+        side_row = pl.multiple_of((to_group * half + lax.rem(to_member, half)) * TOKENS, TOKENS)
+        return (
+            (grad_k.at[pl.ds(row, TOKENS)], key_out.at[side, :, narrow], 0),
+            (grad_v.at[pl.ds(row, TOKENS)], value_out.at[side, :, narrow], 1),
+            (grad_q.at[pl.ds(side_row, TOKENS)], query_out.at[:, wide], 2),
+        )
+
+    def send(piece, to_group, to_member):
+        source, target, which = piece
+        pltpu.make_async_remote_copy(
+            src_ref=source,
+            dst_ref=target,
+            send_sem=send_sem.at[which],
+            recv_sem=recv_sem.at[which],
+            device_id=(to_group, to_member),
+            device_id_type=MESH,
+        ).start()
+
+    @pl.loop(1, everyone)
+    def _(apart):
+        to_group = lax.rem(group + apart // members, groups)
+        to_member = lax.rem(member + lax.rem(apart, members), members)
+        of_key, of_value, of_query = pieces(to_group, to_member)
+        send(of_key, to_group, to_member)
+        send(of_value, to_group, to_member)
+
+        @pl.when(to_member // half == side)
+        def _():
+            send(of_query, to_group, to_member)
+
+    for source, target, which in pieces(group, member):
+        pltpu.make_async_copy(source, target, recv_sem.at[which]).start()
+    others = (everyone - 1) * TOKENS
+    near_others = (groups * half - 1) * TOKENS
+    wait_bytes(grad_k.at[pl.ds(0, others)], send_sem.at[0])
+    wait_bytes(grad_v.at[pl.ds(0, others)], send_sem.at[1])
+    wait_bytes(grad_q.at[pl.ds(0, near_others)], send_sem.at[2])
+    wait_bytes(key_out, recv_sem.at[0])
+    wait_bytes(value_out, recv_sem.at[1])
+    wait_bytes(query_out, recv_sem.at[2])
+
+
+def dot(left, right, dims):
+    return lax.dot_general(left, right, (dims, ((), ())), preferred_element_type=jnp.float32)
+
+
+def attention_kernel(
+    span,
+    inner,
+    scalars,
+    query_all,
+    grad_all,
+    key_all,
+    value_all,
+    stat_all,
+    grad_q,
+    grad_k,
+    grad_v,
+    key_turned,
+    sum_q,
+    sum_k,
+    sum_v,
+):
+    side = scalars[inner]
+    per_span = span // 2 // TILE
+    blocks = key_all.shape[0] // TILE
+
+    @pl.loop(0, blocks)
+    def _(block):
+        rows = pl.ds(block * TILE, TILE)
+        key_turned[block] = key_all[rows].T
+        sum_k[rows] = jnp.zeros((TILE, HEAD_SIZE), jnp.float32)
+        sum_v[rows] = jnp.zeros((TILE, HEAD_SIZE), jnp.float32)
+
+    @pl.loop(0, query_all.shape[0] // TILE)
+    def _(tile):
+        first = (tile // per_span) * span + side * (span // 2) + lax.rem(tile, per_span) * TILE
+        rows = pl.ds(tile * TILE, TILE)
+        query = jnp.concatenate([query_all[rows, :HEAD_SIZE], query_all[rows, HEAD_SIZE:]], 0)
+        grad = jnp.concatenate([grad_all[rows, :HEAD_SIZE], grad_all[rows, HEAD_SIZE:]], 0)
+        parts = TILE // TOKENS
+        stat = [stat_all[tile * parts + part] for part in range(parts)]
+        norm = jnp.concatenate([s[h : h + 1] for h in (0, 1) for s in stat], 1)
+        delta = jnp.concatenate([s[h : h + 1] for h in (2, 3) for s in stat], 1)
+        spot = first + lax.rem(lax.broadcasted_iota(jnp.int32, (1, 2 * TILE), 1), TILE)
+        begin = jnp.zeros((1, 2 * TILE), jnp.int32)
+        lowest = jnp.int32(0)
+        for cut in range(inner):
+            bound = scalars[cut]
+            begin = jnp.where(spot >= bound, bound, begin)
+            lowest = jnp.where(first >= bound, bound, lowest)
+        sum_q[...] = jnp.zeros_like(sum_q)
+
+        @pl.loop(lowest // TILE, first // TILE + 1)
+        def _(block):
+            cols = pl.ds(pl.multiple_of(block * TILE, TILE), TILE)
+            score = dot(key_all[cols], query, ((1,), (1,)))
+            where = block * TILE + lax.broadcasted_iota(jnp.int32, (TILE, 2 * TILE), 0)
+            allowed = (where >= begin) & (where <= spot)
+            prob = jnp.where(allowed, jnp.exp2(score * (attn_scale * math.log2(math.e)) - norm), 0.0)
+            dprob = dot(value_all[cols], grad, ((1,), (1,)))
+            dscore = (prob * (dprob - delta)).astype(jnp.bfloat16)
+            sum_v[cols] += dot(prob.astype(jnp.bfloat16), grad, ((1,), (0,)))
+            sum_k[cols] += dot(dscore, query, ((1,), (0,)))
+            sum_q[...] += dot(key_turned[block], dscore, ((1,), (0,)))
+
+        for head in (0, 1):
+            turned = (sum_q[:, head * TILE : (head + 1) * TILE] * attn_scale).T
+            grad_q[rows, head * HEAD_SIZE : (head + 1) * HEAD_SIZE] = turned.astype(jnp.bfloat16)
+
+    @pl.loop(0, blocks)
+    def _(block):
+        rows = pl.ds(block * TILE, TILE)
+        grad_k[rows] = (sum_k[rows] * attn_scale).astype(jnp.bfloat16)
+        grad_v[rows] = sum_v[rows].astype(jnp.bfloat16)
+
+
+def half_shards(
+    groups, members, query, key_matrix, value_matrix, output_gradient, attn_out, doc_offsets, stats
+):
+    half = members // 2
+    slots = groups * half
+    token_count = groups * members * TOKENS
+    low, wide = jnp.bfloat16, jnp.float32
+    delta = jnp.sum(
+        (output_gradient.astype(wide) * attn_out.astype(wide)).reshape(TOKENS, HQ, HEAD_SIZE),
+        axis=2,
+    )
+    norm = stats * math.log2(math.e)
+    stat = jnp.concatenate(
+        [
+            norm.T.reshape(slots, 2, TOKENS),
+            delta.T.reshape(slots, 2, TOKENS),
+            jnp.zeros((slots, 4, TOKENS), wide),
+        ],
+        1,
+    )
+    anywhere = pl.BlockSpec(memory_space=pl.ANY)
+    near_rows = slots * TOKENS
+    spread = pl.pallas_call(
+        functools.partial(spread_kernel, groups, members),
+        out_shape=(
+            jax.ShapeDtypeStruct((near_rows, 2 * HEAD_SIZE), low),
+            jax.ShapeDtypeStruct((near_rows, 2 * HEAD_SIZE), low),
+            jax.ShapeDtypeStruct((token_count, HEAD_SIZE), low),
+            jax.ShapeDtypeStruct((token_count, HEAD_SIZE), low),
+            jax.ShapeDtypeStruct((slots, 8, TOKENS), wide),
+        ),
+        in_specs=[anywhere] * 5,
+        out_specs=[anywhere] * 5,
+        scratch_shapes=[pltpu.SemaphoreType.DMA((5,)), pltpu.SemaphoreType.DMA((5,))],
+        compiler_params=pltpu.CompilerParams(collective_id=0, has_side_effects=True),
+        name="spread",
+    )(query, output_gradient, key_matrix, value_matrix, stat)
+    inner = doc_offsets.shape[0] - 2
+    side = lax.axis_index("head") // half
+    scalars = jnp.concatenate([doc_offsets[1:-1], side.astype(jnp.int32)[None]])
+    in_vmem = pl.BlockSpec(memory_space=pltpu.VMEM)
+    grad_q, grad_k, grad_v = pl.pallas_call(
+        functools.partial(attention_kernel, members * TOKENS, inner),
+        out_shape=(
+            jax.ShapeDtypeStruct((near_rows, 2 * HEAD_SIZE), low),
+            jax.ShapeDtypeStruct((token_count, HEAD_SIZE), low),
+            jax.ShapeDtypeStruct((token_count, HEAD_SIZE), low),
+        ),
+        in_specs=[pl.BlockSpec(memory_space=pltpu.SMEM)] + [in_vmem] * 5,
+        out_specs=[in_vmem] * 3,
+        scratch_shapes=[
+            pltpu.VMEM((token_count // TILE, HEAD_SIZE, TILE), low),
+            pltpu.VMEM((HEAD_SIZE, 2 * TILE), wide),
+            pltpu.VMEM((token_count, HEAD_SIZE), wide),
+            pltpu.VMEM((token_count, HEAD_SIZE), wide),
+        ],
+        compiler_params=pltpu.CompilerParams(vmem_limit_bytes=40 * 1024 * 1024),
+        name="attention",
+    )(scalars, *spread)
+    grad_query, key_halves, value_halves = pl.pallas_call(
+        functools.partial(collect_kernel, groups, members),
+        out_shape=(
+            jax.ShapeDtypeStruct((TOKENS, HQ * HEAD_SIZE), low),
+            jax.ShapeDtypeStruct((2, TOKENS, slots * HEAD_SIZE), low),
+            jax.ShapeDtypeStruct((2, TOKENS, slots * HEAD_SIZE), low),
+        ),
+        in_specs=[anywhere] * 3,
+        out_specs=[anywhere] * 3,
+        scratch_shapes=[pltpu.SemaphoreType.DMA((3,)), pltpu.SemaphoreType.DMA((3,))],
+        compiler_params=pltpu.CompilerParams(collective_id=1, has_side_effects=True),
+        name="collect",
+    )(grad_q, grad_k, grad_v)
+    key_gradient = (key_halves[0].astype(wide) + key_halves[1].astype(wide)).astype(low)
+    value_gradient = (value_halves[0].astype(wide) + value_halves[1].astype(wide)).astype(low)
+    return (grad_query, key_gradient, value_gradient)
+
+
 def solution(mesh):
     placed = (
         P(("seq", "head"), None),
@@ -197,10 +521,22 @@
         P(),
         P(("seq", "head"), None),
     )
-    return jax.shard_map(
-        shards,
-        mesh=mesh,
-        in_specs=placed,
-        out_specs=(P(("seq", "head"), None), P(("seq", "head"), None), P(("seq", "head"), None)),
-        check_vma=False,
-    )
+    groups, members = mesh.shape["seq"], mesh.shape["head"]
+    halves_fit = members % 2 == 0 and groups * (members // 2) * 2 == HQ
+
+    def whole(*arrays):
+        tokens = arrays[0].shape[0] // (groups * members)
+        fits = halves_fit and tokens == TOKENS and tokens * members == 2 * DOCHALF
+        body = functools.partial(half_shards, groups, members) if fits else shards
+        return mapped(body)(*arrays)
+
+    def mapped(body):
+        return jax.shard_map(
+            body,
+            mesh=mesh,
+            in_specs=placed,
+            out_specs=(P(("seq", "head"), None), P(("seq", "head"), None), P(("seq", "head"), None)),
+            check_vma=False,
+        )
+
+    return whole

time: 243 us -> 168 us (0.69); the launches traced: 238 us -> 166 us
  Pallas kernels: 0 us -> 148 us
  waiting for transfers between devices: 100 us -> 0 us
  starting transfers between devices: 49.8 us -> 0 us
  matrix products: 35.3 us -> 0 us
  local copies, waits for them, and re-layouts: 40.6 us -> 10.9 us
  other arithmetic: 10.8 us -> 6.89 us
    pallas_call x0 -> x3, Pallas kernels: none -> 148 us  [the longest x1 73.9 us: half_shards(): pl.pallas_call(functools.partial(spread_kernel, groups, members), out_sha...]
    all_to_all x9 -> x0, waiting for transfers between devices: 78.2 us -> none  [the longest x1 23.9 us: shards(): lax.all_to_all(query, 'head', split_axis=1, concat_axis=0, tiled=True)]
    all_to_all x9 -> x0, starting transfers between devices: 40.1 us -> none  [the longest x1 6.55 us: shards(): lax.all_to_all(query_low, 'head', split_axis=0, concat_axis=1, tiled=True)]
    dot_general x10 -> x0, matrix products: 35.3 us -> none  [the longest x2 16.2 us: tile_grads(): jnp.einsum('qgrd,kgd->grqk', grad_rows, value_window, preferred_element_t...]
    ppermute x4 -> x0, waiting for transfers between devices: 22.3 us -> none  [from_behind(): lax.ppermute(value, axis, [(source, source + steps) for source in range(l...]
    ppermute x4 -> x0, starting transfers between devices: 9.69 us -> none  [from_behind(): lax.ppermute(value, axis, [(source, source + steps) for source in range(l...]
    while x32 -> x0, local copies, waits for them, and re-layouts: 9.4 us -> none
    all_to_all x10 -> x0, local copies, waits for them, and re-layouts: 6.72 us -> none  [the longest x2 2.11 us: shards(): lax.all_to_all(query_low, 'head', split_axis=0, concat_axis=1, tiled=True)]
  transfers between devices with their start and end apart: 13 -> 0, of which waited for: 12 -> 0; matrix products, arithmetic and copies ran while one was open for 12% -> 0% of each run, Pallas kernels for 0% -> 0%
where the time goes in v1:
time: 168 us; the launch traced here: 166 us
  Pallas kernels  148 us (88%)
  local copies, waits for them, and re-layouts  10.9 us (6%)
  other arithmetic  6.89 us (4%)
    pallas_call x1, Pallas kernels, half_shards(): pl.pallas_call(functools.partial(spread_kernel, groups, members), out_sha...  73.9 us
    pallas_call x1, Pallas kernels, half_shards(): pl.pallas_call(functools.partial(collect_kernel, groups, members), out_sh...  62.2 us
    pallas_call x1, Pallas kernels, half_shards(): pl.pallas_call(functools.partial(attention_kernel, members * TOKENS, inne...  11.8 us
    unnamed x20, local copies, waits for them, and re-layouts  10 us

profile of v1, /device:TPU:4, one launch (start us, length us, event | category | flops | bytes accessed | tf_op | source)
XLA Modules:
  0.0 166.5 jit_solution(5753654802381289390)
XLA Ops:
  0.6 0.7 slice.15
  1.4 0.1 pad_add_fusion.scalars
  1.5 0.1 pad.2.clone
  1.5 0.7 broadcast_multiply_fusion
  2.2 1.8 %multiply_bitcast_fusion = f32[16,8,32,128]{3,1,2,0:T(8,128)S(1)} fusion(bf16[128,4096]{1,0:T(8,128)(2,1)} %param.11, bf16[128,4096]{1,0:T(8,128)(2,1)} %grad.1), kind=kLoop, calls=%fused_computation | loop fusion | flops 1572864 | bytes 4194304
  4.1 0.4 copy.11
  4.4 0.6 reduce_sum.9
  5.0 0.1 copy.10
  5.1 0.7 maximum_maximum_fusion.stat
  5.8 73.9 %spread.1 = (bf16[2048,256]{1,0:T(8,128)(2,1)}, bf16[2048,256]{1,0:T(8,128)(2,1)}, bf16[4096,128]{1,0:T(8,128)(2,1)}, bf16[4096,128]{1,0:T(8,128)(2,1)}, f32[16,8,128]{2,1,0:T(8,128)}) custom-call(bf16[128,4096]{1,0:T(8,128)(2,1)} %query.1, bf16[128,4096]{1,0:T(8,128)(2,1)} %grad.1, bf16[128,2048]{1,0:T(8,128)(2,1)} %key.1, bf16[128,2048]{1,0:T(8,128)(2,1)} %value.1, ...), custom_call_target="tpu_custom_call" | custom-call | tf_op jit(solution)/shard_map/spread/pallas_call | solution.py:459
  79.8 0.0 copy-start.3
  79.8 1.2 copy-done.3
  81.0 0.0 copy-start.4
  81.0 1.2 copy-done.4
  82.2 0.0 copy-start.5
  82.2 1.2 copy-done.5
  83.5 0.0 copy-start.6
  83.5 1.2 copy-done.6
  84.7 0.0 copy-start.7
  84.7 0.8 copy-done.7
  85.5 11.8 %attention.1 = (bf16[2048,256]{1,0:T(8,128)(2,1)S(1)}, bf16[4096,128]{1,0:T(8,128)(2,1)S(1)}, bf16[4096,128]{1,0:T(8,128)(2,1)S(1)}) custom-call(s32[8]{0:T(128)S(1)} %pad_add_fusion.scalars, bf16[2048,256]{1,0:T(8,128)(2,1)S(1)} %copy-done.3, bf16[2048,256]{1,0:T(8,128)(2,1)S(1)} %copy-done.4, bf16[4096,128]{1,0:T(8,128)(2,1)S(1)} %copy-done.5, ...), custom_call_target="tpu_custom_call" | custom-call | tf_op jit(solution)/shard_map/attention/pallas_call | solution.py:478
  97.4 0.0 copy-start
  97.4 1.0 copy-done
  98.3 0.0 copy-start.1
  98.3 1.0 copy-done.1
  99.3 0.0 copy-start.2
  99.3 1.0 copy-done.2
  100.3 62.2 %collect.1 = (bf16[128,4096]{1,0:T(8,128)(2,1)}, bf16[2,128,2048]{2,1,0:T(8,128)(2,1)}, bf16[2,128,2048]{2,1,0:T(8,128)(2,1)}) custom-call(bf16[2048,256]{1,0:T(8,128)(2,1)} %copy-done, bf16[4096,128]{1,0:T(8,128)(2,1)} %copy-done.1, bf16[4096,128]{1,0:T(8,128)(2,1)} %copy-done.2), custom_call_target="tpu_custom_call" | custom-call | tf_op jit(solution)/shard_map/collect/pallas_call | solution.py:496
  162.5 0.0 copy-start.8
  162.6 3.0 %fusion = (bf16[128,2048]{1,0:T(8,128)(2,1)}, bf16[128,2048]{1,0:T(8,128)(2,1)}) fusion(bf16[2,128,2048]{2,1,0:T(8,128)(2,1)} %get-tuple-element.23, bf16[2,128,2048]{2,1,0:T(8,128)(2,1)} %get-tuple-element.24), kind=kLoop, calls=%fused_computation.3 | loop fusion | flops 2097152 | bytes 3145728 | tf_op jit(solution)/shard_map/convert_element_type | solution.py:509
  165.5 0.0 copy-done.8
  165.5 1.0 copy.13
  (1 shorter events, 0.0 us)
Async XLA Ops:
  79.8 1.2 copy-start.3
  81.0 1.2 copy-start.4
  82.2 1.2 copy-start.5
  83.5 1.2 copy-start.6
  84.7 0.8 copy-start.7
  97.4 1.0 copy-start
  98.3 1.0 copy-start.1
  99.3 1.0 copy-start.2
  162.5 3.0 %copy-start.8 = (bf16[128,4096]{1,0:T(8,128)(2,1)S(1)}, bf16[128,4096]{1,0:T(8,128)(2,1)}, u32[]{:S(2)}) copy-start(bf16[128,4096]{1,0:T(8,128)(2,1)} %get-tuple-element.30) | copy-start | bytes 3145732

commit v2 on v0

--- a/solution.py
+++ b/solution.py
@@ -1,6 +1,11 @@
+import functools
+import math
+
 import jax
 import jax.numpy as jnp
 from jax import lax
+from jax.experimental import pallas as pl
+from jax.experimental.pallas import tpu as pltpu
 from jax.sharding import PartitionSpec as P
 
 HQ = 32
@@ -187,6 +192,350 @@
     return (grad_query, key_gradient, value_gradient)
 
 
+TOKENS = 128
+TILE = 256
+PHASE = 8
+MESH = pl.DeviceIdType.MESH
+
+
+def wait_bytes(ref, sem):
+    pltpu.make_async_copy(ref, ref, sem).wait()
+
+
+def greet_all(groups, members, group, member):
+    barrier = pltpu.get_barrier_semaphore()
+    everyone = groups * members
+
+    @pl.loop(1, everyone)
+    def _(apart):
+        to_group = lax.rem(group + apart // members, groups)
+        to_member = lax.rem(member + lax.rem(apart, members), members)
+        pl.semaphore_signal(barrier, inc=1, device_id=(to_group, to_member), device_id_type=MESH)
+
+    pl.semaphore_wait(barrier, everyone - 1)
+
+
+def fused_kernel(
+    groups,
+    members,
+    inner,
+    offsets,
+    query,
+    grad,
+    key,
+    value,
+    attn_out,
+    norm,
+    query_out,
+    key_out,
+    value_out,
+    query_all,
+    grad_all,
+    key_all,
+    value_all,
+    stat_all,
+    grad_own,
+    out_own,
+    stat_own,
+    grad_q,
+    grad_k,
+    grad_v,
+    key_turned,
+    sum_q,
+    sum_k,
+    sum_v,
+    send_sem,
+    recv_sem,
+    own_sem,
+):
+    half = members // 2
+    everyone = groups * members
+    group = lax.axis_index("seq")
+    member = lax.axis_index("head")
+    side = member // half
+    greet_all(groups, members, group, member)
+    token_row = pl.multiple_of((group * members + member) * TOKENS, TOKENS)
+    side_slot = group * half + lax.rem(member, half)
+    side_row = pl.multiple_of(side_slot * TOKENS, TOKENS)
+
+    def pieces(slot):
+        narrow = pl.ds(pl.multiple_of(slot * HEAD_SIZE, HEAD_SIZE), HEAD_SIZE)
+        wide = pl.ds(pl.multiple_of(slot * 2 * HEAD_SIZE, 2 * HEAD_SIZE), 2 * HEAD_SIZE)
+        far = (
+            (key.at[:, narrow], key_all.at[pl.ds(token_row, TOKENS)], 0),
+            (value.at[:, narrow], value_all.at[pl.ds(token_row, TOKENS)], 1),
+        )
+        near = (
+            (query.at[:, wide], query_all.at[pl.ds(side_row, TOKENS)], 2),
+            (grad.at[:, wide], grad_all.at[pl.ds(side_row, TOKENS)], 3),
+            (stat_own.at[slot], stat_all.at[side_slot], 4),
+        )
+        return far, near
+
+    def send(piece, to_group, to_member):
+        source, target, which = piece
+        pltpu.make_async_remote_copy(
+            src_ref=source,
+            dst_ref=target,
+            send_sem=send_sem.at[which],
+            recv_sem=recv_sem.at[which],
+            device_id=(to_group, to_member),
+            device_id_type=MESH,
+        ).start()
+
+    @pl.loop(0, groups * half)
+    def _(step):
+        turn = lax.rem(step + lax.rem(group, 2) * PHASE, groups * half)
+        to_group = lax.rem(group + turn // half, groups)
+        to_local = lax.rem(member + lax.rem(turn, half), half)
+        slot = to_group * half + to_local
+        far, near = pieces(slot)
+        here = (to_group, side * half + to_local)
+        across = (to_group, (1 - side) * half + to_local)
+
+        @pl.when(turn > 0)
+        def _():
+            send(far[0], *here)
+            send(far[1], *here)
+
+        send(far[0], *across)
+
+        @pl.when(turn > 0)
+        def _():
+            send(near[0], *here)
+
+        send(far[1], *across)
+
+        @pl.when(turn > 0)
+        def _():
+            send(near[1], *here)
+
+    load_grad = pltpu.make_async_copy(grad, grad_own, own_sem.at[0])
+    load_out = pltpu.make_async_copy(attn_out, out_own, own_sem.at[1])
+    load_grad.start()
+    load_out.start()
+    load_grad.wait()
+    load_out.wait()
+    for slot in range(groups * half):
+        for part in range(2):
+            head = 2 * slot + part
+            columns = slice(head * HEAD_SIZE, (head + 1) * HEAD_SIZE)
+            both = grad_own[:, columns].astype(jnp.float32) * out_own[:, columns].astype(jnp.float32)
+            stat_own[slot, 2 + part : 3 + part] = jnp.sum(both.T, axis=0, keepdims=True)
+            stat_own[slot, part : part + 1] = norm[head : head + 1] * math.log2(math.e)
+        stat_own[slot, 4:8] = jnp.zeros((4, TOKENS), jnp.float32)
+
+    far, near = pieces(side_slot)
+    for source, target, which in far + near[:2]:
+        pltpu.make_async_copy(source, target, recv_sem.at[which]).start()
+    others = (everyone - 1) * TOKENS
+    near_others = (groups * half - 1) * TOKENS
+    wait_bytes(key_all.at[pl.ds(0, others)], send_sem.at[0])
+
+    @pl.loop(1, groups * half)
+    def _(turn):
+        to_group = lax.rem(group + turn // half, groups)
+        to_local = lax.rem(member + lax.rem(turn, half), half)
+        send(pieces(to_group * half + to_local)[1][2], to_group, side * half + to_local)
+
+    pltpu.make_async_copy(stat_own.at[side_slot], stat_all.at[side_slot], recv_sem.at[4]).start()
+    wait_bytes(key_all, recv_sem.at[0])
+
+    @pl.loop(0, key_all.shape[0] // TILE)
+    def _(block):
+        rows = pl.ds(pl.multiple_of(block * TILE, TILE), TILE)
+        key_turned[block] = key_all[rows].T
+        sum_k[rows] = jnp.zeros((TILE, HEAD_SIZE), jnp.float32)
+        sum_v[rows] = jnp.zeros((TILE, HEAD_SIZE), jnp.float32)
+
+    wait_bytes(value_all, recv_sem.at[1])
+    wait_bytes(query_all, recv_sem.at[2])
+    wait_bytes(grad_all, recv_sem.at[3])
+    wait_bytes(stat_all, recv_sem.at[4])
+    span = members * TOKENS
+    per_span = span // 2 // TILE
+    parts = TILE // TOKENS
+    narrow = pl.ds(pl.multiple_of(side_slot * HEAD_SIZE, HEAD_SIZE), HEAD_SIZE)
+    wide = pl.ds(pl.multiple_of(side_slot * 2 * HEAD_SIZE, 2 * HEAD_SIZE), 2 * HEAD_SIZE)
+
+    def compute(at_group, tile):
+        first = at_group * span + side * (span // 2) + tile * TILE
+        slot = at_group * half + tile * parts
+        rows = pl.ds(pl.multiple_of(slot * TOKENS, TOKENS), TILE)
+        queries = jnp.concatenate([query_all[rows, :HEAD_SIZE], query_all[rows, HEAD_SIZE:]], 0)
+        grads = jnp.concatenate([grad_all[rows, :HEAD_SIZE], grad_all[rows, HEAD_SIZE:]], 0)
+        stat = [stat_all[slot + part] for part in range(parts)]
+        level = jnp.concatenate([s[h : h + 1] for h in (0, 1) for s in stat], 1)
+        delta = jnp.concatenate([s[h : h + 1] for h in (2, 3) for s in stat], 1)
+        spot = first + lax.rem(lax.broadcasted_iota(jnp.int32, (1, 2 * TILE), 1), TILE)
+        begin = jnp.zeros((1, 2 * TILE), jnp.int32)
+        for cut in range(inner):
+            bound = offsets[cut + 1]
+            begin = jnp.where(spot >= bound, bound, begin)
+        sum_q[...] = jnp.zeros_like(sum_q)
+        back_blocks = span // TILE
+
+        @pl.loop(0, back_blocks + 1)
+        def _(step):
+            block = first // TILE + step - back_blocks
+
+            @pl.when(block >= 0)
+            def _():
+                cols = pl.ds(pl.multiple_of(block * TILE, TILE), TILE)
+                score = dot(key_all[cols], queries, ((1,), (1,)))
+                where = block * TILE + lax.broadcasted_iota(jnp.int32, (TILE, 2 * TILE), 0)
+                allowed = (where >= begin) & (where <= spot)
+                power = jnp.exp2(score * (attn_scale * math.log2(math.e)) - level)
+                prob = jnp.where(allowed, power, 0.0)
+                dprob = dot(value_all[cols], grads, ((1,), (1,)))
+                dscore = (prob * (dprob - delta)).astype(jnp.bfloat16)
+                sum_v[cols] += dot(prob.astype(jnp.bfloat16), grads, ((1,), (0,)))
+                sum_k[cols] += dot(dscore, queries, ((1,), (0,)))
+                sum_q[...] += dot(key_turned[block], dscore, ((1,), (0,)))
+
+        for part in (0, 1):
+            turned = (sum_q[:, part * TILE : (part + 1) * TILE] * attn_scale).T
+            grad_q[rows, part * HEAD_SIZE : (part + 1) * HEAD_SIZE] = turned.astype(jnp.bfloat16)
+
+    def give(piece, to_group, to_member):
+        mine = (to_group == group) & (to_member == member)
+
+        @pl.when(mine)
+        def _():
+            source, target, which = piece
+            pltpu.make_async_copy(source, target, recv_sem.at[which]).start()
+
+        @pl.when(jnp.logical_not(mine))
+        def _():
+            send(piece, to_group, to_member)
+
+    def give_query(at_group, tile):
+        for part in range(parts):
+            local = tile * parts + part
+            row = pl.multiple_of((at_group * half + local) * TOKENS, TOKENS)
+            piece = (grad_q.at[pl.ds(row, TOKENS)], query_out.at[:, wide], 5)
+            give(piece, at_group, side * half + local)
+
+    def each_owner(chunk, act):
+        @pl.loop(0, members)
+        def _(step):
+            owner = (chunk - 1) * members + side * half + lax.rem(step + member, members)
+
+            @pl.when((owner >= 0) & (owner < everyone))
+            def _():
+                act(owner, pl.ds(pl.multiple_of(owner * TOKENS, TOKENS), TOKENS))
+
+    def settle(owner, rows):
+        grad_k[rows] = (sum_k[rows] * attn_scale).astype(jnp.bfloat16)
+        grad_v[rows] = sum_v[rows].astype(jnp.bfloat16)
+
+    def give_key(owner, rows):
+        to_group, to_member = owner // members, lax.rem(owner, members)
+        give((grad_k.at[rows], key_out.at[side, :, narrow], 6), to_group, to_member)
+        give((grad_v.at[rows], value_out.at[side, :, narrow], 7), to_group, to_member)
+
+    def finished(turn, act):
+        at_group = lax.rem(group + turn, groups)
+
+        @pl.when((turn > 0) | (at_group == 0))
+        def _():
+            each_owner(at_group, act)
+
+        @pl.when(at_group == groups - 1)
+        def _():
+            each_owner(groups, act)
+
+        @pl.when((turn == groups - 1) & (group > 0))
+        def _():
+            each_owner(group, act)
+
+    @pl.loop(0, groups)
+    def _(turn):
+        at_group = lax.rem(group + turn, groups)
+
+        @pl.loop(0, per_span)
+        def _(part):
+            tile = lax.rem(part + lax.rem(member, half) // 2, per_span)
+            compute(at_group, tile)
+
+            @pl.when(part > 0)
+            def _():
+                give_query(at_group, lax.rem(tile + per_span - 1, per_span))
+
+            @pl.when((part == 0) & (turn > 0))
+            def _():
+                finished(turn - 1, give_key)
+
+        finished(turn, settle)
+        last = lax.rem(per_span - 1 + lax.rem(member, half) // 2, per_span)
+        give_query(at_group, last)
+
+    finished(groups - 1, give_key)
+    wait_bytes(value_all.at[pl.ds(0, others)], send_sem.at[1])
+    wait_bytes(query_all.at[pl.ds(0, near_others)], send_sem.at[2])
+    wait_bytes(grad_all.at[pl.ds(0, near_others)], send_sem.at[3])
+    wait_bytes(stat_all.at[pl.ds(0, groups * half - 1)], send_sem.at[4])
+    wait_bytes(grad_q.at[pl.ds(0, near_others)], send_sem.at[5])
+    wait_bytes(grad_k.at[pl.ds(0, others)], send_sem.at[6])
+    wait_bytes(grad_v.at[pl.ds(0, others)], send_sem.at[7])
+    wait_bytes(query_out, recv_sem.at[5])
+    wait_bytes(key_out, recv_sem.at[6])
+    wait_bytes(value_out, recv_sem.at[7])
+
+
+def dot(left, right, dims):
+    return lax.dot_general(left, right, (dims, ((), ())), preferred_element_type=jnp.float32)
+
+
+def half_shards(
+    groups, members, query, key_matrix, value_matrix, output_gradient, attn_out, doc_offsets, stats
+):
+    slots = groups * (members // 2)
+    token_count = groups * members * TOKENS
+    near_rows = slots * TOKENS
+    low, wide = jnp.bfloat16, jnp.float32
+    in_vmem = pl.BlockSpec(memory_space=pltpu.VMEM)
+    in_smem = pl.BlockSpec(memory_space=pltpu.SMEM)
+    anywhere = pl.BlockSpec(memory_space=pl.ANY)
+    grad_query, key_halves, value_halves = pl.pallas_call(
+        functools.partial(fused_kernel, groups, members, doc_offsets.shape[0] - 2),
+        out_shape=(
+            jax.ShapeDtypeStruct((TOKENS, HQ * HEAD_SIZE), low),
+            jax.ShapeDtypeStruct((2, TOKENS, slots * HEAD_SIZE), low),
+            jax.ShapeDtypeStruct((2, TOKENS, slots * HEAD_SIZE), low),
+        ),
+        in_specs=[in_smem] + [anywhere] * 5 + [in_vmem],
+        out_specs=[anywhere] * 3,
+        scratch_shapes=[
+            pltpu.VMEM((near_rows, 2 * HEAD_SIZE), low),
+            pltpu.VMEM((near_rows, 2 * HEAD_SIZE), low),
+            pltpu.VMEM((token_count, HEAD_SIZE), low),
+            pltpu.VMEM((token_count, HEAD_SIZE), low),
+            pltpu.VMEM((slots, 8, TOKENS), wide),
+            pltpu.VMEM((TOKENS, HQ * HEAD_SIZE), low),
+            pltpu.VMEM((TOKENS, HQ * HEAD_SIZE), low),
+            pltpu.VMEM((slots, 8, TOKENS), wide),
+            pltpu.VMEM((near_rows, 2 * HEAD_SIZE), low),
+            pltpu.VMEM((token_count, HEAD_SIZE), low),
+            pltpu.VMEM((token_count, HEAD_SIZE), low),
+            pltpu.VMEM((token_count // TILE, HEAD_SIZE, TILE), low),
+            pltpu.VMEM((HEAD_SIZE, 2 * TILE), wide),
+            pltpu.VMEM((token_count, HEAD_SIZE), wide),
+            pltpu.VMEM((token_count, HEAD_SIZE), wide),
+            pltpu.SemaphoreType.DMA((8,)),
+            pltpu.SemaphoreType.DMA((8,)),
+            pltpu.SemaphoreType.DMA((2,)),
+        ],
+        compiler_params=pltpu.CompilerParams(
+            collective_id=0, has_side_effects=True
+        ),
+        name="fused",
+    )(doc_offsets, query, output_gradient, key_matrix, value_matrix, attn_out, stats.T)
+    key_gradient = (key_halves[0].astype(wide) + key_halves[1].astype(wide)).astype(low)
+    value_gradient = (value_halves[0].astype(wide) + value_halves[1].astype(wide)).astype(low)
+    return (grad_query, key_gradient, value_gradient)
+
+
 def solution(mesh):
     placed = (
         P(("seq", "head"), None),
@@ -197,10 +546,22 @@
         P(),
         P(("seq", "head"), None),
     )
-    return jax.shard_map(
-        shards,
-        mesh=mesh,
-        in_specs=placed,
-        out_specs=(P(("seq", "head"), None), P(("seq", "head"), None), P(("seq", "head"), None)),
-        check_vma=False,
-    )
+    groups, members = mesh.shape["seq"], mesh.shape["head"]
+    halves_fit = members % 2 == 0 and groups * (members // 2) * 2 == HQ
+
+    def whole(*arrays):
+        tokens = arrays[0].shape[0] // (groups * members)
+        fits = halves_fit and tokens == TOKENS and tokens * members == 2 * DOCHALF
+        body = functools.partial(half_shards, groups, members) if fits else shards
+        return mapped(body)(*arrays)
+
+    def mapped(body):
+        return jax.shard_map(
+            body,
+            mesh=mesh,
+            in_specs=placed,
+            out_specs=(P(("seq", "head"), None), P(("seq", "head"), None), P(("seq", "head"), None)),
+            check_vma=False,
+        )
+
+    return whole

time: 243 us -> 136 us (0.56); the launches traced: 238 us -> 136 us
  Pallas kernels: 0 us -> 132 us
  waiting for transfers between devices: 100 us -> 0 us
  starting transfers between devices: 49.8 us -> 0 us
  local copies, waits for them, and re-layouts: 40.6 us -> 0.97 us
  matrix products: 35.3 us -> 0 us
  other arithmetic: 10.8 us -> 2.97 us
    pallas_call x0 -> x1, Pallas kernels: none -> 132 us  [half_shards(): pl.pallas_call(functools.partial(fused_kernel, groups, members, doc_offse...]
    all_to_all x9 -> x0, waiting for transfers between devices: 78.2 us -> none  [the longest x1 23.9 us: shards(): lax.all_to_all(query, 'head', split_axis=1, concat_axis=0, tiled=True)]
    all_to_all x9 -> x0, starting transfers between devices: 40.1 us -> none  [the longest x1 6.55 us: shards(): lax.all_to_all(query_low, 'head', split_axis=0, concat_axis=1, tiled=True)]
    dot_general x10 -> x0, matrix products: 35.3 us -> none  [the longest x2 16.2 us: tile_grads(): jnp.einsum('qgrd,kgd->grqk', grad_rows, value_window, preferred_element_t...]
    ppermute x4 -> x0, waiting for transfers between devices: 22.3 us -> none  [from_behind(): lax.ppermute(value, axis, [(source, source + steps) for source in range(l...]
    unnamed x27 -> x3, local copies, waits for them, and re-layouts: 11.8 us -> 0.97 us
    ppermute x4 -> x0, starting transfers between devices: 9.69 us -> none  [from_behind(): lax.ppermute(value, axis, [(source, source + steps) for source in range(l...]
    while x32 -> x0, local copies, waits for them, and re-layouts: 9.4 us -> none
  transfers between devices with their start and end apart: 13 -> 0, of which waited for: 12 -> 0; matrix products, arithmetic and copies ran while one was open for 12% -> 0% of each run, Pallas kernels for 0% -> 0%
where the time goes in v2:
time: 136 us
  Pallas kernels  132 us (97%)
  other arithmetic  2.97 us (2%)
    pallas_call x1, Pallas kernels, half_shards(): pl.pallas_call(functools.partial(fused_kernel, groups, members, doc_offse...  132 us
    convert_element_type x1, other arithmetic, half_shards(): (key_halves[0].astype(wide) + key_halves[1].astype(wide)).astype(low)  2.97 us

profile of v2, /device:TPU:4, one launch (start us, length us, event | category | flops | bytes accessed | tf_op | source)
XLA Modules:
  0.0 136.2 jit_solution(1200709741021758207)
XLA Ops:
  0.6 131.6 %fused.1 = (bf16[128,4096]{1,0:T(8,128)(2,1)}, bf16[2,128,2048]{2,1,0:T(8,128)(2,1)}, bf16[2,128,2048]{2,1,0:T(8,128)(2,1)}) custom-call(s32[9]{0:T(128)} %offsets.1, bf16[128,4096]{1,0:T(8,128)(2,1)} %query.1, bf16[128,4096]{1,0:T(8,128)(2,1)} %grad.1, bf16[128,2048]{1,0:T(8,128)(2,1)} %key.1, bf16[128,2048]{1,0:T(8,128)(2,1)} %value.1, ...), custom_call_target="tpu_custom_call" | custom-call | tf_op jit(solution)/shard_map/fused/pallas_call | solution.py:500
  132.2 0.0 copy-start
  132.2 3.0 %fusion = (bf16[128,2048]{1,0:T(8,128)(2,1)}, bf16[128,2048]{1,0:T(8,128)(2,1)}) fusion(bf16[2,128,2048]{2,1,0:T(8,128)(2,1)} %get-tuple-element.7, bf16[2,128,2048]{2,1,0:T(8,128)(2,1)} %get-tuple-element.8), kind=kLoop, calls=%fused_computation.2 | loop fusion | flops 2097152 | bytes 3145728 | tf_op jit(solution)/shard_map/convert_element_type | solution.py:534
  135.2 0.0 copy-done
  135.2 1.0 copy.11
Async XLA Ops:
  132.2 3.0 %copy-start = (bf16[128,4096]{1,0:T(8,128)(2,1)S(1)}, bf16[128,4096]{1,0:T(8,128)(2,1)}, u32[]{:S(2)}) copy-start(bf16[128,4096]{1,0:T(8,128)(2,1)} %get-tuple-element.14) | copy-start | bytes 3145732

commit v3 on v2

--- a/solution.py
+++ b/solution.py
@@ -194,7 +194,6 @@
 
 TOKENS = 128
 TILE = 256
-PHASE = 8
 MESH = pl.DeviceIdType.MESH
 
 
@@ -272,44 +271,51 @@
         )
         return far, near
 
+    def slot_of(which):
+        return group if which < 5 else 0
+
     def send(piece, to_group, to_member):
         source, target, which = piece
         pltpu.make_async_remote_copy(
             src_ref=source,
             dst_ref=target,
             send_sem=send_sem.at[which],
-            recv_sem=recv_sem.at[which],
+            recv_sem=recv_sem.at[which, slot_of(which)],
             device_id=(to_group, to_member),
             device_id_type=MESH,
         ).start()
 
-    @pl.loop(0, groups * half)
-    def _(step):
-        turn = lax.rem(step + lax.rem(group, 2) * PHASE, groups * half)
-        to_group = lax.rem(group + turn // half, groups)
-        to_local = lax.rem(member + lax.rem(turn, half), half)
-        slot = to_group * half + to_local
-        far, near = pieces(slot)
-        here = (to_group, side * half + to_local)
-        across = (to_group, (1 - side) * half + to_local)
-
-        @pl.when(turn > 0)
-        def _():
-            send(far[0], *here)
-            send(far[1], *here)
-
-        send(far[0], *across)
-
-        @pl.when(turn > 0)
-        def _():
-            send(near[0], *here)
-
-        send(far[1], *across)
-
-        @pl.when(turn > 0)
-        def _():
-            send(near[1], *here)
-
+    def send_group(apart, keys, queries):
+        to_group = lax.rem(group + apart, groups)
+
+        @pl.loop(0, half)
+        def _(step):
+            to_local = lax.rem(member + step, half)
+            far, near = pieces(to_group * half + to_local)
+            here = (to_group, side * half + to_local)
+            across = (to_group, (1 - side) * half + to_local)
+            other = (apart > 0) | (step > 0)
+            if keys:
+
+                @pl.when(other)
+                def _():
+                    send(far[0], *here)
+                    send(far[1], *here)
+
+                send(far[0], *across)
+                send(far[1], *across)
+            if queries:
+
+                @pl.when(other)
+                def _():
+                    send(near[0], *here)
+                    send(near[1], *here)
+
+    far, near = pieces(side_slot)
+    for source, target, which in far + near[:2]:
+        pltpu.make_async_copy(source, target, recv_sem.at[which, group]).start()
+    send_group(0, True, True)
+    send_group(1, True, False)
     load_grad = pltpu.make_async_copy(grad, grad_own, own_sem.at[0])
     load_out = pltpu.make_async_copy(attn_out, out_own, own_sem.at[1])
     load_grad.start()
@@ -325,12 +331,7 @@
             stat_own[slot, part : part + 1] = norm[head : head + 1] * math.log2(math.e)
         stat_own[slot, 4:8] = jnp.zeros((4, TOKENS), jnp.float32)
 
-    far, near = pieces(side_slot)
-    for source, target, which in far + near[:2]:
-        pltpu.make_async_copy(source, target, recv_sem.at[which]).start()
-    others = (everyone - 1) * TOKENS
-    near_others = (groups * half - 1) * TOKENS
-    wait_bytes(key_all.at[pl.ds(0, others)], send_sem.at[0])
+    send_group(groups - 1, True, False)
 
     @pl.loop(1, groups * half)
     def _(turn):
@@ -338,20 +339,15 @@
         to_local = lax.rem(member + lax.rem(turn, half), half)
         send(pieces(to_group * half + to_local)[1][2], to_group, side * half + to_local)
 
-    pltpu.make_async_copy(stat_own.at[side_slot], stat_all.at[side_slot], recv_sem.at[4]).start()
-    wait_bytes(key_all, recv_sem.at[0])
-
-    @pl.loop(0, key_all.shape[0] // TILE)
-    def _(block):
-        rows = pl.ds(pl.multiple_of(block * TILE, TILE), TILE)
-        key_turned[block] = key_all[rows].T
-        sum_k[rows] = jnp.zeros((TILE, HEAD_SIZE), jnp.float32)
-        sum_v[rows] = jnp.zeros((TILE, HEAD_SIZE), jnp.float32)
-
-    wait_bytes(value_all, recv_sem.at[1])
-    wait_bytes(query_all, recv_sem.at[2])
-    wait_bytes(grad_all, recv_sem.at[3])
-    wait_bytes(stat_all, recv_sem.at[4])
+    keep = pltpu.make_async_copy(stat_own.at[side_slot], stat_all.at[side_slot], recv_sem.at[4, group])
+    keep.start()
+    send_group(groups - 1, False, True)
+    for apart in range(groups - 2, 1, -1):
+        send_group(apart, True, True)
+    send_group(1, False, True)
+    others = (everyone - 1) * TOKENS
+    near_others = (groups * half - 1) * TOKENS
+
     span = members * TOKENS
     per_span = span // 2 // TILE
     parts = TILE // TOKENS
@@ -403,7 +399,7 @@
         @pl.when(mine)
         def _():
             source, target, which = piece
-            pltpu.make_async_copy(source, target, recv_sem.at[which]).start()
+            pltpu.make_async_copy(source, target, recv_sem.at[which, 0]).start()
 
         @pl.when(jnp.logical_not(mine))
         def _():
@@ -449,9 +445,39 @@
         def _():
             each_owner(group, act)
 
+    def arrive_keys(at_group):
+        whole = pl.ds(pl.multiple_of(at_group * span, span), span)
+        wait_bytes(key_all.at[whole], recv_sem.at[0, at_group])
+        wait_bytes(value_all.at[whole], recv_sem.at[1, at_group])
+
+        @pl.loop(0, span // TILE)
+        def _(part):
+            block = at_group * (span // TILE) + part
+            rows = pl.ds(pl.multiple_of(block * TILE, TILE), TILE)
+            key_turned[block] = key_all[rows].T
+            sum_k[rows] = jnp.zeros((TILE, HEAD_SIZE), jnp.float32)
+            sum_v[rows] = jnp.zeros((TILE, HEAD_SIZE), jnp.float32)
+
+    def arrive_queries(at_group):
+        near_span = half * TOKENS
+        rows = pl.ds(pl.multiple_of(at_group * near_span, near_span), near_span)
+        wait_bytes(query_all.at[rows], recv_sem.at[2, at_group])
+        wait_bytes(grad_all.at[rows], recv_sem.at[3, at_group])
+        wait_bytes(stat_all.at[pl.ds(at_group * half, half)], recv_sem.at[4, at_group])
+
     @pl.loop(0, groups)
     def _(turn):
         at_group = lax.rem(group + turn, groups)
+
+        @pl.when((turn < groups - 1) | (group == 0))
+        def _():
+            arrive_keys(at_group)
+
+        @pl.when((turn == 0) & (group > 0))
+        def _():
+            arrive_keys(group - 1)
+
+        arrive_queries(at_group)
 
         @pl.loop(0, per_span)
         def _(part):
@@ -471,6 +497,7 @@
         give_query(at_group, last)
 
     finished(groups - 1, give_key)
+    wait_bytes(key_all.at[pl.ds(0, others)], send_sem.at[0])
     wait_bytes(value_all.at[pl.ds(0, others)], send_sem.at[1])
     wait_bytes(query_all.at[pl.ds(0, near_others)], send_sem.at[2])
     wait_bytes(grad_all.at[pl.ds(0, near_others)], send_sem.at[3])
@@ -478,9 +505,9 @@
     wait_bytes(grad_q.at[pl.ds(0, near_others)], send_sem.at[5])
     wait_bytes(grad_k.at[pl.ds(0, others)], send_sem.at[6])
     wait_bytes(grad_v.at[pl.ds(0, others)], send_sem.at[7])
-    wait_bytes(query_out, recv_sem.at[5])
-    wait_bytes(key_out, recv_sem.at[6])
-    wait_bytes(value_out, recv_sem.at[7])
+    wait_bytes(query_out, recv_sem.at[5, 0])
+    wait_bytes(key_out, recv_sem.at[6, 0])
+    wait_bytes(value_out, recv_sem.at[7, 0])
 
 
 def dot(left, right, dims):
@@ -523,7 +550,7 @@
             pltpu.VMEM((token_count, HEAD_SIZE), wide),
             pltpu.VMEM((token_count, HEAD_SIZE), wide),
             pltpu.SemaphoreType.DMA((8,)),
-            pltpu.SemaphoreType.DMA((8,)),
+            pltpu.SemaphoreType.DMA((8, groups)),
             pltpu.SemaphoreType.DMA((2,)),
         ],
         compiler_params=pltpu.CompilerParams(
@@ -547,7 +574,7 @@
         P(("seq", "head"), None),
     )
     groups, members = mesh.shape["seq"], mesh.shape["head"]
-    halves_fit = members % 2 == 0 and groups * (members // 2) * 2 == HQ
+    halves_fit = groups > 2 and members % 2 == 0 and groups * (members // 2) * 2 == HQ
 
     def whole(*arrays):
         tokens = arrays[0].shape[0] // (groups * members)

time: 136 us -> 123 us (0.904); the launches traced: 136 us -> 121 us
  Pallas kernels: 132 us -> 116 us
    pallas_call x1, Pallas kernels: 132 us -> 116 us  [half_shards(): pl.pallas_call(functools.partial(fused_kernel, groups, members, doc_offse...]
where the time goes in v3:
time: 123 us; the launch traced here: 121 us
  Pallas kernels  116 us (94%)
  other arithmetic  2.97 us (2%)
    pallas_call x1, Pallas kernels, half_shards(): pl.pallas_call(functools.partial(fused_kernel, groups, members, doc_offse...  116 us
    convert_element_type x1, other arithmetic, half_shards(): (key_halves[0].astype(wide) + key_halves[1].astype(wide)).astype(low)  2.97 us

profile of v3, /device:TPU:4, one launch (start us, length us, event | category | flops | bytes accessed | tf_op | source)
XLA Modules:
  0.0 120.9 jit_solution(18346499628243380778)
XLA Ops:
  0.6 116.3 %fused.1 = (bf16[128,4096]{1,0:T(8,128)(2,1)}, bf16[2,128,2048]{2,1,0:T(8,128)(2,1)}, bf16[2,128,2048]{2,1,0:T(8,128)(2,1)}) custom-call(s32[9]{0:T(128)} %offsets.1, bf16[128,4096]{1,0:T(8,128)(2,1)} %query.1, bf16[128,4096]{1,0:T(8,128)(2,1)} %grad.1, bf16[128,2048]{1,0:T(8,128)(2,1)} %key.1, bf16[128,2048]{1,0:T(8,128)(2,1)} %value.1, ...), custom_call_target="tpu_custom_call" | custom-call | tf_op jit(solution)/shard_map/fused/pallas_call | solution.py:527
  116.9 0.0 copy-start
  116.9 3.0 %fusion = (bf16[128,2048]{1,0:T(8,128)(2,1)}, bf16[128,2048]{1,0:T(8,128)(2,1)}) fusion(bf16[2,128,2048]{2,1,0:T(8,128)(2,1)} %get-tuple-element.7, bf16[2,128,2048]{2,1,0:T(8,128)(2,1)} %get-tuple-element.8), kind=kLoop, calls=%fused_computation.2 | loop fusion | flops 2097152 | bytes 3145728 | tf_op jit(solution)/shard_map/convert_element_type | solution.py:561
  119.9 0.0 copy-done
  119.9 1.0 copy.11
Async XLA Ops:
  116.9 3.0 %copy-start = (bf16[128,4096]{1,0:T(8,128)(2,1)S(1)}, bf16[128,4096]{1,0:T(8,128)(2,1)}, u32[]{:S(2)}) copy-start(bf16[128,4096]{1,0:T(8,128)(2,1)} %get-tuple-element.14) | copy-start | bytes 3145732

commit v4 on v3

--- a/solution.py
+++ b/solution.py
@@ -253,6 +253,7 @@
     member = lax.axis_index("head")
     side = member // half
     greet_all(groups, members, group, member)
+    tail_rows = (group == groups - 1) & (side == 1)
     token_row = pl.multiple_of((group * members + member) * TOKENS, TOKENS)
     side_slot = group * half + lax.rem(member, half)
     side_row = pl.multiple_of(side_slot * TOKENS, TOKENS)
@@ -302,8 +303,11 @@
                     send(far[0], *here)
                     send(far[1], *here)
 
-                send(far[0], *across)
-                send(far[1], *across)
+                @pl.when(jnp.logical_not(tail_rows))
+                def _():
+                    send(far[0], *across)
+                    send(far[1], *across)
+
             if queries:
 
                 @pl.when(other)
@@ -417,7 +421,7 @@
         def _(step):
             owner = (chunk - 1) * members + side * half + lax.rem(step + member, members)
 
-            @pl.when((owner >= 0) & (owner < everyone))
+            @pl.when((owner >= 0) & (owner < everyone - (1 - side) * half))
             def _():
                 act(owner, pl.ds(pl.multiple_of(owner * TOKENS, TOKENS), TOKENS))
 
@@ -447,14 +451,28 @@
 
     def arrive_keys(at_group):
         whole = pl.ds(pl.multiple_of(at_group * span, span), span)
-        wait_bytes(key_all.at[whole], recv_sem.at[0, at_group])
-        wait_bytes(value_all.at[whole], recv_sem.at[1, at_group])
+        first_half = pl.ds(pl.multiple_of(at_group * span, span), span // 2)
+        part_only = (at_group == groups - 1) & (side == 0)
+
+        @pl.when(part_only)
+        def _():
+            wait_bytes(key_all.at[first_half], recv_sem.at[0, at_group])
+            wait_bytes(value_all.at[first_half], recv_sem.at[1, at_group])
+
+        @pl.when(jnp.logical_not(part_only))
+        def _():
+            wait_bytes(key_all.at[whole], recv_sem.at[0, at_group])
+            wait_bytes(value_all.at[whole], recv_sem.at[1, at_group])
 
         @pl.loop(0, span // TILE)
         def _(part):
             block = at_group * (span // TILE) + part
             rows = pl.ds(pl.multiple_of(block * TILE, TILE), TILE)
-            key_turned[block] = key_all[rows].T
+
+            @pl.when(jnp.logical_not(part_only) | (part < span // TILE // 2))
+            def _():
+                key_turned[block] = key_all[rows].T
+
             sum_k[rows] = jnp.zeros((TILE, HEAD_SIZE), jnp.float32)
             sum_v[rows] = jnp.zeros((TILE, HEAD_SIZE), jnp.float32)
 
@@ -497,17 +515,40 @@
         give_query(at_group, last)
 
     finished(groups - 1, give_key)
-    wait_bytes(key_all.at[pl.ds(0, others)], send_sem.at[0])
-    wait_bytes(value_all.at[pl.ds(0, others)], send_sem.at[1])
+    for which, ref in enumerate((key_all, value_all)):
+
+        @pl.when(tail_rows)
+        def _():
+            wait_bytes(ref.at[pl.ds(0, near_others)], send_sem.at[which])
+
+        @pl.when(jnp.logical_not(tail_rows))
+        def _():
+            wait_bytes(ref.at[pl.ds(0, others)], send_sem.at[which])
+
     wait_bytes(query_all.at[pl.ds(0, near_others)], send_sem.at[2])
     wait_bytes(grad_all.at[pl.ds(0, near_others)], send_sem.at[3])
     wait_bytes(stat_all.at[pl.ds(0, groups * half - 1)], send_sem.at[4])
     wait_bytes(grad_q.at[pl.ds(0, near_others)], send_sem.at[5])
-    wait_bytes(grad_k.at[pl.ds(0, others)], send_sem.at[6])
-    wait_bytes(grad_v.at[pl.ds(0, others)], send_sem.at[7])
+    for which, ref in ((6, grad_k), (7, grad_v)):
+
+        @pl.when(side == 0)
+        def _():
+            wait_bytes(ref.at[pl.ds(0, others - half * TOKENS)], send_sem.at[which])
+
+        @pl.when(side == 1)
+        def _():
+            wait_bytes(ref.at[pl.ds(0, others)], send_sem.at[which])
+
     wait_bytes(query_out, recv_sem.at[5, 0])
-    wait_bytes(key_out, recv_sem.at[6, 0])
-    wait_bytes(value_out, recv_sem.at[7, 0])
+    for which, ref in ((6, key_out), (7, value_out)):
+
+        @pl.when(tail_rows)
+        def _():
+            wait_bytes(ref.at[1], recv_sem.at[which, 0])
+
+        @pl.when(jnp.logical_not(tail_rows))
+        def _():
+            wait_bytes(ref, recv_sem.at[which, 0])
 
 
 def dot(left, right, dims):
@@ -558,8 +599,12 @@
         ),
         name="fused",
     )(doc_offsets, query, output_gradient, key_matrix, value_matrix, attn_out, stats.T)
-    key_gradient = (key_halves[0].astype(wide) + key_halves[1].astype(wide)).astype(low)
-    value_gradient = (value_halves[0].astype(wide) + value_halves[1].astype(wide)).astype(low)
+    lone = (lax.axis_index("seq") == groups - 1) & (lax.axis_index("head") >= members // 2)
+
+    def total(halves):
+        return (jnp.where(lone, 0.0, halves[0].astype(wide)) + halves[1].astype(wide)).astype(low)
+
+    key_gradient, value_gradient = total(key_halves), total(value_halves)
     return (grad_query, key_gradient, value_gradient)
 
 

time: 123 us -> 122 us (level)
  no operation moved by 1% of the time
where the time goes in v4:
time: 122 us; the launch traced here: 120 us
  Pallas kernels  116 us (95%)
  other arithmetic  2.96 us (2%)
    pallas_call x1, Pallas kernels, half_shards(): pl.pallas_call(functools.partial(fused_kernel, groups, members, doc_offse...  116 us
    convert_element_type x1, other arithmetic, total(): (jnp.where(lone, 0.0, halves[0].astype(wide)) + halves[1].astype(wide)).a...  2.96 us

profile of v4, /device:TPU:4, one launch (start us, length us, event | category | flops | bytes accessed | tf_op | source)
XLA Modules:
  0.0 120.3 jit_solution(11213973961613933757)
XLA Ops:
  0.6 115.7 %fused.1 = (bf16[128,4096]{1,0:T(8,128)(2,1)}, bf16[2,128,2048]{2,1,0:T(8,128)(2,1)}, bf16[2,128,2048]{2,1,0:T(8,128)(2,1)}) custom-call(s32[9]{0:T(128)} %offsets.1, bf16[128,4096]{1,0:T(8,128)(2,1)} %query.1, bf16[128,4096]{1,0:T(8,128)(2,1)} %grad.1, bf16[128,2048]{1,0:T(8,128)(2,1)} %key.1, bf16[128,2048]{1,0:T(8,128)(2,1)} %value.1, ...), custom_call_target="tpu_custom_call" | custom-call | tf_op jit(solution)/shard_map/fused/pallas_call | solution.py:568
  116.4 0.0 copy-start
  116.4 3.0 %fusion = (bf16[128,2048]{1,0:T(8,128)(2,1)}, bf16[128,2048]{1,0:T(8,128)(2,1)}) fusion(bf16[2,128,2048]{2,1,0:T(8,128)(2,1)} %get-tuple-element.7, pred[]{:T(512)S(6)} %and.5, bf16[2,128,2048]{2,1,0:T(8,128)(2,1)} %get-tuple-element.8), kind=kLoop, calls=%fused_computation.2 | loop fusion | flops 2621440 | bytes 3145729 | tf_op jit(solution)/shard_map/convert_element_type | solution.py:605
  119.3 0.0 copy-done
  119.3 1.0 copy.11
Async XLA Ops:
  116.4 3.0 %copy-start = (bf16[128,4096]{1,0:T(8,128)(2,1)S(1)}, bf16[128,4096]{1,0:T(8,128)(2,1)}, u32[]{:S(2)}) copy-start(bf16[128,4096]{1,0:T(8,128)(2,1)} %get-tuple-element.14) | copy-start | bytes 3145732
